TPU v7x, 32 devices: a 4x4x1 block of a 4x4x8 slice. The times are simulated.
32 devices in a mesh: rep: 2 (over z, core), dp: 16 (over x, y).
Axes of the slice: x: 4, y: 4, z: 1, core: 2. Of those that a mesh axis runs over, the one named last changes fastest.
The devices are a block of a 4x4x8 slice.
Arguments:
- x: bfloat16 [32, 1024, 512], P(('rep', 'dp')), parts along dimension 0
- dy: bfloat16 [32, 1024, 512], P(('rep', 'dp')), parts along dimension 0
- w_gate: bfloat16 [2, 512, 8192], replicated
- w_up: bfloat16 [2, 512, 8192], replicated
- w_down: bfloat16 [2, 8192, 512], replicated
- m_w_gate: float32 [2, 512, 8192], P(None, 'dp')
- m_w_up: float32 [2, 512, 8192], P(None, 'dp')
- m_w_down: float32 [2, 8192, 512], P(None, 'dp')
- v_w_gate: float32 [2, 512, 8192], P(None, 'dp')
- v_w_up: float32 [2, 512, 8192], P(None, 'dp')
- v_w_down: float32 [2, 8192, 512], P(None, 'dp')
Outputs:
- output 1: bfloat16 [4, 512, 8192], P('rep'), parts along dimension 0
- output 2: bfloat16 [4, 512, 8192], P('rep'), parts along dimension 0
- output 3: bfloat16 [4, 8192, 512], P('rep'), parts along dimension 0
- output 4: float32 [4, 512, 8192], P('rep', 'dp'), parts along dimension 0
- output 5: float32 [4, 512, 8192], P('rep', 'dp'), parts along dimension 0
- output 6: float32 [4, 8192, 512], P('rep', 'dp'), parts along dimension 0
- output 7: float32 [4, 512, 8192], P('rep', 'dp'), parts along dimension 0
- output 8: float32 [4, 512, 8192], P('rep', 'dp'), parts along dimension 0
- output 9: float32 [4, 8192, 512], P('rep', 'dp'), parts along dimension 0
There are 2 independent parts. A program takes and returns all parts, laid end to end along the dimension named above; an argument that names none is the same for every part.
All inputs are finite; a program needn't handle non-finite values.
Results may differ from a plain program's by a relative error of at most 0.022.
Values are sent between devices in bfloat16 or wider.
A program may use at most 768 MiB of HBM per device.

v0:
```python
import jax
import jax.numpy as jnp
from jax import lax

NAMES = ("w_gate", "w_up", "w_down")


def matmul(a, w):
    return jnp.dot(a, w, preferred_element_type=jnp.float32).astype(jnp.bfloat16)


def normed(h):
    wide = h.astype(jnp.float32)
    scale = lax.rsqrt(jnp.mean(wide**2, -1, keepdims=True) + 1e-6)
    return (wide * scale).astype(jnp.bfloat16)


def layer(h, w):
    a = normed(h)
    gate = jnp.dot(a, w["w_gate"], preferred_element_type=jnp.float32)
    up = jnp.dot(a, w["w_up"], preferred_element_type=jnp.float32)
    return h + matmul((jax.nn.silu(gate) * up).astype(jnp.bfloat16), w["w_down"])


def adamw(w, m, v, g):
    m = 0.9 * m + 0.1 * g
    v = 0.95 * v + 0.05 * g * g
    step = m * lax.rsqrt(v + 1e-8) + 0.1 * w
    return (w - 0.02 * step).astype(jnp.bfloat16), m, v


def clipped(gradients, sum_of_squares, count):
    factor = jnp.minimum(1.0, 0.5 * lax.rsqrt(sum_of_squares / count + 1e-30))
    return [g * factor for g in gradients]


def stack(weights, h):
    for number in range(weights["w_gate"].shape[0]):
        h = layer(h, {name: w[number] for name, w in weights.items()})
    return h


def solution(mesh):
    groups = mesh.shape["rep"]

    def step(x, dy, *arrays):
        weights, m, v = (arrays[i : i + 3] for i in (0, 3, 6))
        x, dy = (t.reshape(groups, -1, *t.shape[1:]) for t in (x, dy))

        def of_a_group(x, dy):
            _, back = jax.vjp(lambda w: stack(w, x), dict(zip(NAMES, weights, strict=True)))
            by_weights = back(dy)[0]
            gradients = [by_weights[name].astype(jnp.float32) for name in NAMES]
            gradients = clipped(gradients, sum(jnp.sum(g * g) for g in gradients), sum(g.size for g in gradients))
            new = [adamw(w.astype(jnp.float32), m, v, g) for w, m, v, g in zip(weights, m, v, gradients, strict=True)]
            return tuple(one[which] for which in range(3) for one in new)

        return tuple(t.reshape(-1, *t.shape[2:]) for t in jax.vmap(of_a_group)(x, dy))

    return step
```

profile of v0, /device:TPU:96, one launch (start us, length us, event | category | flops | bytes accessed | tf_op | source)
XLA Modules:
  0.0 1295.1 jit_solution(15243300188081018685)
XLA Ops:
  7.2 0.1 reduce-scatter.29.cloned.1.call-start
  7.3 1.5 fusion.82
  8.8 1.5 copy
  10.3 19.3 %fusion.60 = f32[1024,8192]{1,0:T(8,128)} fusion(bf16[2,512,8192]{2,1,0:T(8,128)(2,1)} %param, bf16[1,1024,512]{2,1,0:T(8,128)(2,1)} %param.2, f32[1024]{0:T(1024)S(1)} %add_rsqrt_fusion), kind=kOutput, calls=%fused_computation.64 | convolution fusion | flops 8591507456 | bytes 42995712 | tf_op jit(solution)/vmap(jvp())/dot_general | solution.py:20
  29.6 18.0 %fusion.58 = f32[1024,8192]{1,0:T(8,128)} fusion(bf16[2,512,8192]{2,1,0:T(8,128)(2,1)} %param.3, bf16[1,1024,512]{2,1,0:T(8,128)(2,1)S(1)} %copy-done.3, f32[1024]{0:T(1024)S(1)} %add_rsqrt_fusion), kind=kOutput, calls=%fused_computation.62 | convolution fusion | flops 8591507456 | bytes 42995712 | tf_op jit(solution)/vmap(jvp())/dot_general | solution.py:21
  47.6 27.4 %fusion.26 = bf16[1024,8192]{1,0:T(8,128)(2,1)} fusion(f32[1024,8192]{1,0:T(8,128)} %fusion.58, f32[1024,8192]{1,0:T(8,128)} %fusion.60), kind=kLoop, calls=%fused_computation.35 | loop fusion | flops 50331648 | bytes 83886080
  75.0 14.9 %fusion.102 = (f32[1024]{0:T(1024)S(1)}, bf16[1,1,1024,512]{2,3,1,0:T(8,128)(2,1)S(1)}) fusion(bf16[1024,8192]{1,0:T(8,128)(2,1)} %fusion.26, bf16[2,8192,512]{2,1,0:T(8,128)(2,1)} %param.4, bf16[1,1024,512]{1,2,0:T(8,128)(2,1)S(1)} %copy), kind=kOutput, calls=%fused_computation.128 | convolution fusion | flops 8592555008 | bytes 27267072 | tf_op jit(solution)/vmap(jvp())/dot_general | solution.py:9
  90.0 19.1 %fusion.47 = f32[1024,8192]{1,0:T(8,128)} fusion(bf16[2,512,8192]{2,1,0:T(8,128)(2,1)} %param, bf16[1,1,1024,512]{2,3,1,0:T(8,128)(2,1)S(1)} %get-tuple-element.10, f32[1024]{0:T(1024)S(1)} %bitcast.371), kind=kOutput, calls=%fused_computation.51 | convolution fusion | flops 8591507456 | bytes 42995712 | tf_op jit(solution)/vmap(jvp())/dot_general | solution.py:20
  109.1 18.8 %fusion.51 = f32[1024,8192]{1,0:T(8,128)} fusion(bf16[2,512,8192]{2,1,0:T(8,128)(2,1)} %param.3, bf16[1,1,1024,512]{2,3,1,0:T(8,128)(2,1)S(1)} %get-tuple-element.10, f32[1024]{0:T(1024)S(1)} %bitcast.372), kind=kOutput, calls=%fused_computation.55 | convolution fusion | flops 8591507456 | bytes 42995712 | tf_op jit(solution)/vmap(jvp())/dot_general | solution.py:21
  127.9 15.2 %convolution_convert_fusion.1 = bf16[1024,8192]{1,0:T(8,128)(2,1)} fusion(bf16[2,8192,512]{2,1,0:T(8,128)(2,1)} %param.4, bf16[1,1024,512]{2,1,0:T(8,128)(2,1)S(1)} %copy-done.6), kind=kOutput, calls=%fused_computation.44 | convolution fusion | flops 8598323200 | bytes 26214400 | tf_op jit(solution)/vmap(transpose(jvp()))/dot_general | solution.py:9
  143.2 0.5 copy.1
  143.7 33.4 %fusion.6 = bf16[1024,8192]{1,0:T(8,128)(2,1)} fusion(f32[1024,8192]{1,0:T(8,128)} %fusion.47, f32[1024,8192]{1,0:T(8,128)} %fusion.51, bf16[1024,8192]{1,0:T(8,128)(2,1)} %convolution_convert_fusion.1), kind=kLoop, calls=%fused_computation.11 | loop fusion | flops 100663296 | bytes 100663296
  177.1 15.6 %fusion.108 = bf16[1024,512]{0,1:T(8,128)(2,1)} fusion(bf16[1024,8192]{1,0:T(8,128)(2,1)} %fusion.6, bf16[2,512,8192]{2,1,0:T(8,128)(2,1)} %param), kind=kOutput, calls=%fused_computation.133 | convolution fusion | flops 8589934592 | bytes 26214400 | tf_op jit(solution)/vmap(transpose(jvp()))/dot_general | solution.py:20
  192.7 24.3 %fusion.104 = (f32[1024]{0:T(1024)S(1)}, bf16[1,1,1024,512]{2,3,1,0:T(8,128)(2,1)}) fusion(bf16[1,1,1024,512]{2,3,1,0:T(8,128)(2,1)S(1)} %get-tuple-element.10, bf16[1024,512]{0,1:T(8,128)(2,1)} %fusion.108, bf16[2,512,8192]{2,1,0:T(8,128)(2,1)} %param.3, bf16[1024,8192]{1,0:T(8,128)(2,1)} %convolution_convert_fusion.1, f32[1024,8192]{1,0:T(8,128)} %fusion.47), kind=kOutput, calls=%fused_computation.130 | convolution fusion | flops 8643410944 | bytes 61870080 | tf_op jit(solution)/vmap(transpose(jvp()))/dot_general | solution.py:21
  217.0 1.9 fusion.138
  219.0 1.0 copy-done.9
  219.9 16.0 %convolution_bitcast_fusion = f32[1,8192,512]{2,1,0:T(8,128)} fusion(bf16[1024,8192]{1,0:T(8,128)(2,1)} %fusion.26, bf16[1024,512]{0,1:T(8,128)(2,1)S(1)} %fusion.138), kind=kOutput, calls=%fused_computation.49 | convolution fusion | flops 8589934592 | bytes 34603008 | tf_op jit(solution)/vmap(transpose(jvp()))/dot_general | solution.py:9
  235.9 0.1 reduce-scatter.29.cloned.1.call-update
  236.0 0.1 reduce-scatter.27.cloned.1.call-start
  236.1 29.4 %fusion.35 = f32[1,8192,512]{2,1,0:T(8,128)} fusion(f32[1024,8192]{1,0:T(8,128)} %fusion.51, f32[1024,8192]{1,0:T(8,128)} %fusion.47, bf16[1,1024,512]{2,1,0:T(8,128)(2,1)S(1)} %copy-done.6), kind=kOutput, calls=%fused_computation.45 | convolution fusion | flops 8640266240 | bytes 84934656 | tf_op jit(solution)/vmap(transpose(jvp()))/dot_general | solution.py:9
  265.5 0.1 reduce-scatter.27.cloned.1.call-update
  265.6 0.1 reduce-scatter.25.cloned.1.call-start
  265.7 1.1 copy-done.10
  266.7 16.2 %convolution_convert_fusion = bf16[1024,8192]{1,0:T(8,128)(2,1)} fusion(bf16[1024,512]{0,1:T(8,128)(2,1)S(1)} %copy-done.10, bf16[2,8192,512]{2,1,0:T(8,128)(2,1)} %param.4), kind=kOutput, calls=%fused_computation.43 | convolution fusion | flops 8598323200 | bytes 26214400 | tf_op jit(solution)/vmap(transpose(jvp()))/dot_general | solution.py:9
  282.9 25.6 %fusion.44 = f32[1,512,8192]{2,1,0:T(8,128)} fusion(bf16[1024,8192]{1,0:T(8,128)(2,1)} %convolution_convert_fusion, f32[1024,8192]{1,0:T(8,128)} %fusion.60, bf16[1,1024,512]{1,2,0:T(8,128)(2,1)S(1)} %copy-done.8, f32[1024]{0:T(1024)S(1)} %copy-done.12), kind=kOutput, calls=%fused_computation.48 | convolution fusion | flops 8641839104 | bytes 68161536 | tf_op jit(solution)/vmap(transpose(jvp()))/dot_general | solution.py:21
  308.6 0.1 reduce-scatter.23.cloned.1.call-start
  308.6 1.1 copy-done.2
  309.7 25.8 %fusion.38 = f32[1,512,8192]{2,1,0:T(8,128)} fusion(bf16[1024,8192]{1,0:T(8,128)(2,1)} %convolution_convert_fusion.1, f32[1024,8192]{1,0:T(8,128)} %fusion.47, bf16[1,1,1024,512]{2,3,1,0:T(8,128)(2,1)S(1)} %copy-done.2, f32[1024]{0:T(1024)S(1)} %bitcast.374), kind=kOutput, calls=%fused_computation.46 | convolution fusion | flops 8641839104 | bytes 68161536 | tf_op jit(solution)/vmap(transpose(jvp()))/dot_general | solution.py:21
  335.5 0.1 reduce-scatter.23.cloned.1.call-update
  335.6 0.1 reduce-scatter.21.cloned.1.call-start
  335.7 35.8 %fusion.41 = f32[1,512,8192]{2,1,0:T(8,128)} fusion(f32[1024,8192]{1,0:T(8,128)} %fusion.60, f32[1024,8192]{1,0:T(8,128)} %fusion.58, bf16[1024,8192]{1,0:T(8,128)(2,1)} %convolution_convert_fusion, bf16[1,1024,512]{1,2,0:T(8,128)(2,1)S(1)} %copy-done.8, f32[1024]{0:T(1024)S(1)} %copy-done.12), kind=kOutput, calls=%fused_computation.47 | convolution fusion | flops 8683782144 | bytes 101715968 | tf_op jit(solution)/vmap(transpose(jvp()))/dot_general | solution.py:20
  371.6 0.1 reduce-scatter.19.cloned.1.call-start
  371.6 15.8 %convolution_bitcast_fusion.1 = f32[1,512,8192]{2,1,0:T(8,128)} fusion(bf16[1024,8192]{1,0:T(8,128)(2,1)} %fusion.6, bf16[1,1,1024,512]{2,3,1,0:T(8,128)(2,1)S(1)} %copy-done.2, f32[1024]{0:T(1024)S(1)} %bitcast.375), kind=kOutput, calls=%fused_computation.50 | convolution fusion | flops 8591507456 | bytes 34607104 | tf_op jit(solution)/vmap(transpose(jvp()))/dot_general | solution.py:20
  387.5 0.4 all-gather.14.cloned.1.call-start
  387.9 0.2 copy-done.13
  388.1 0.6 dynamic-slice
  389.4 1.3 convert_bitcast_fusion.3
  390.7 61.8 %reduce-scatter.27.cloned.1.call-done = f32[1,512,512]{2,1,0:T(8,128)} async-done(((f32[1,8192,512]{2,1,0:T(8,128)}), f32[1,512,512]{2,1,0:T(8,128)}) %reduce-scatter.27.cloned.1.call-update) | async-done | bytes 1048592
  452.4 1.3 convert_bitcast_fusion.4
  453.7 1.1 fusion.86
  454.9 105.8 %reduce-scatter.25.cloned.1.call-done = f32[1,32,8192]{2,1,0:T(8,128)} async-done(((f32[1,512,8192]{2,1,0:T(8,128)}), f32[1,32,8192]{2,1,0:T(8,128)}) %reduce-scatter.25.cloned.1.call-update) | async-done | bytes 1048592
  560.6 1.3 convert_bitcast_fusion.5
  561.9 106.8 %reduce-scatter.23.cloned.1.call-done = f32[1,32,8192]{2,1,0:T(8,128)} async-done(((f32[1,512,8192]{2,1,0:T(8,128)}), f32[1,32,8192]{2,1,0:T(8,128)}) %reduce-scatter.23.cloned.1.call-update) | async-done | bytes 1048592
  668.7 1.3 convert_bitcast_fusion.6
  670.0 1.1 fusion.85
  671.1 106.2 %reduce-scatter.21.cloned.1.call-done = f32[1,32,8192]{2,1,0:T(8,128)} async-done(((f32[1,512,8192]{2,1,0:T(8,128)}), f32[1,32,8192]{2,1,0:T(8,128)}) %reduce-scatter.21.cloned.1.call-update) | async-done | bytes 1048592
  777.3 1.3 convert_bitcast_fusion.7
  778.6 107.3 %reduce-scatter.19.cloned.1.call-done = f32[1,32,8192]{2,1,0:T(8,128)} async-done(((f32[1,512,8192]{2,1,0:T(8,128)}), f32[1,32,8192]{2,1,0:T(8,128)}) %reduce-scatter.19.cloned.1.call-update) | async-done | bytes 1048592
  885.9 1.3 convert_bitcast_fusion.8
  887.2 1.1 fusion.84
  890.3 39.3 %all-reduce.16 = f32[1]{0:T(128)} all-reduce(f32[1]{0:T(128)} %bitcast.50), channel_id=5, replica_groups=mesh['rep'=2,'dp'=16] {'dp'}, use_global_device_ids=true, to_apply=%region_3.4.clone | all-reduce | flops 1 | bytes 8 | tf_op jit(solution)/vmap()/reduce_sum | solution.py:54
  930.2 6.1 fusion.142
  936.4 0.1 all-gather.12.cloned.1.call-start
  936.4 6.0 fusion.143
  942.5 0.1 all-gather.10.cloned.1.call-start
  942.6 6.0 fusion.144
  948.7 89.4 %all-gather.14.cloned.1.call-done = bf16[1,2,8192,512]{3,2,1,0:T(8,128)(2,1)} async-done(((bf16[1,2,512,512]{3,2,1,0:T(8,128)(2,1)}), bf16[1,2,8192,512]{3,2,1,0:T(8,128)(2,1)}) %all-gather.14.cloned.1.call-update) | async-done | bytes 16777232 | tf_op jit(solution)/reshape | solution.py:58
  1038.1 107.9 %all-gather.12.cloned.1.call-done = bf16[1,2,512,8192]{3,2,1,0:T(8,128)(2,1)} async-done(((bf16[1,2,32,8192]{3,2,1,0:T(8,128)(2,1)}), bf16[1,2,512,8192]{3,2,1,0:T(8,128)(2,1)}) %all-gather.12.cloned.1.call-update) | async-done | bytes 16777232 | tf_op jit(solution)/reshape | solution.py:58
  1146.0 108.0 %all-gather.10.cloned.1.call-done = bf16[1,2,512,8192]{3,2,1,0:T(8,128)(2,1)} async-done(((bf16[1,2,32,8192]{3,2,1,0:T(8,128)(2,1)}), bf16[1,2,512,8192]{3,2,1,0:T(8,128)(2,1)}) %all-gather.10.cloned.1.call-update) | async-done | bytes 16777232 | tf_op jit(solution)/reshape | solution.py:58
  1254.0 16.7 %copy.5 = bf16[2,512,8192]{2,1,0:T(8,128)(2,1)} copy(bf16[2,512,8192]{2,1,0:T(8,128)(2,1)} %bitcast.370) | data formatting | bytes 33554432
  1270.6 8.5 copy.6
  1279.2 1.5 slice-done.2
  1280.7 1.2 slice-done.3
  1281.9 6.2 copy.7
  (42 shorter events, 0.5 us)
Async XLA Ops:
  7.2 382.2 %reduce-scatter.29.cloned.1.call-start = ((), (), s32[]{:S(2)}) async-start(), calls=%async_computation.14 | async-start | bytes 17825792
  10.3 64.8 %copy-start.7 = (bf16[1,1024,512]{1,2,0:T(8,128)(2,1)}, bf16[1,1024,512]{1,2,0:T(8,128)(2,1)S(1)}, u32[]{:S(2)}) copy-start(bf16[1,1024,512]{1,2,0:T(8,128)(2,1)S(1)} %copy) | copy-start | bytes 3145732
  10.3 19.3 %copy-start.11 = (f32[1024]{0:T(1024)}, f32[1024]{0:T(1024)S(1)}, u32[]{:S(2)}) copy-start(f32[1024]{0:T(1024)S(1)} %add_rsqrt_fusion) | copy-start | bytes 12292
  10.3 19.3 %copy-start.3 = (bf16[1,1024,512]{2,1,0:T(8,128)(2,1)S(1)}, bf16[1,1024,512]{2,1,0:T(8,128)(2,1)}, u32[]{:S(2)}) copy-start(bf16[1,1024,512]{2,1,0:T(8,128)(2,1)} %param.2) | copy-start | bytes 3145732
  90.0 127.1 %copy-start.1 = (bf16[1,1,1024,512]{2,3,1,0:T(8,128)(2,1)}, bf16[1,1,1024,512]{2,3,1,0:T(8,128)(2,1)S(1)}, u32[]{:S(2)}) copy-start(bf16[1,1,1024,512]{2,3,1,0:T(8,128)(2,1)S(1)} %get-tuple-element.10) | copy-start | bytes 3145732
  90.0 127.0 %copy-start.4 = (f32[1,1,1024]{2,1,0:T(1,128)}, f32[1,1,1024]{2,1,0:T(1,128)S(1)}, u32[]{:S(2)}) copy-start(f32[1,1,1024]{2,1,0:T(1,128)S(1)} %rsqrt.38) | copy-start | bytes 12292
  109.1 18.8 %copy-start.6 = (bf16[1,1024,512]{2,1,0:T(8,128)(2,1)S(1)}, bf16[1,1024,512]{2,1,0:T(8,128)(2,1)}, u32[]{:S(2)}) copy-start(bf16[1,1024,512]{2,1,0:T(8,128)(2,1)} %param.5) | copy-start | bytes 3145732
  219.0 1.0 copy-start.9
  236.0 216.4 %reduce-scatter.27.cloned.1.call-start = ((), (), s32[]{:S(2)}) async-start(), calls=%async_computation.13 | async-start | bytes 17825792
  265.5 1.2 copy-start.10
  265.6 17.4 %copy-start.8 = (bf16[1,1024,512]{1,2,0:T(8,128)(2,1)S(1)}, bf16[1,1024,512]{1,2,0:T(8,128)(2,1)}, u32[]{:S(2)}) copy-start(bf16[1,1024,512]{1,2,0:T(8,128)(2,1)} %copy-done.7) | copy-start | bytes 3145732
  265.6 17.4 %copy-start.12 = (f32[1024]{0:T(1024)S(1)}, f32[1024]{0:T(1024)}, u32[]{:S(2)}) copy-start(f32[1024]{0:T(1024)} %copy-done.11) | copy-start | bytes 12292
  265.6 295.0 %reduce-scatter.25.cloned.1.call-start = ((), (), s32[]{:S(2)}) async-start(), calls=%async_computation.12 | async-start | bytes 17825792
  308.5 1.2 copy-start.2
  308.5 1.2 copy-start.5
  308.6 360.1 %reduce-scatter.23.cloned.1.call-start = ((), (), s32[]{:S(2)}) async-start(), calls=%async_computation.11 | async-start | bytes 17825792
  335.6 441.7 %reduce-scatter.21.cloned.1.call-start = ((), (), s32[]{:S(2)}) async-start(), calls=%async_computation.10 | async-start | bytes 17825792
  371.6 514.3 %reduce-scatter.19.cloned.1.call-start = ((), (), s32[]{:S(2)}) async-start(), calls=%async_computation.9 | async-start | bytes 17825792
  387.5 0.7 copy-start.13
  387.5 650.5 %all-gather.14.cloned.1.call-start = ((), (), s32[]{:S(2)}) async-start(), calls=%async_computation.8 | async-start | bytes 17825792 | tf_op jit(solution)/reshape | solution.py:58
  936.4 209.6 %all-gather.12.cloned.1.call-start = ((), (), s32[]{:S(2)}) async-start(), calls=%async_computation.7 | async-start | bytes 17825792 | tf_op jit(solution)/reshape | solution.py:58
  942.5 311.4 %all-gather.10.cloned.1.call-start = ((), (), s32[]{:S(2)}) async-start(), calls=%async_computation.6 | async-start | bytes 17825792 | tf_op jit(solution)/reshape | solution.py:58
  1254.0 16.7 %copy-start = (bf16[1,2,512,8192]{3,2,1,0:T(8,128)(2,1)S(1)}, bf16[1,2,512,8192]{3,2,1,0:T(8,128)(2,1)}, u32[]{:S(2)}) copy-start(bf16[1,2,512,8192]{3,2,1,0:T(8,128)(2,1)} %all-gather.12.cloned.1.call-done) | copy-start | bytes 50331652
  1254.0 25.2 %slice-start = ((s8[16777216]{0:T(1024)(128)(4,1)}), s8[4194304]{0:T(1024)(128)(4,1)S(1)}, s32[]{:S(2)}) async-start(s8[16777216]{0:T(1024)(128)(4,1)} %bitcast.366), calls=%async_computation.15 | async-start | bytes 8388608
  1254.0 25.2 %slice-start.1 = ((s8[16777216]{0:T(1024)(128)(4,1)}), s8[4194304]{0:T(1024)(128)(4,1)S(1)}, s32[]{:S(2)}) async-start(s8[16777216]{0:T(1024)(128)(4,1)} %bitcast.366), calls=%async_computation.16 | async-start | bytes 8388608
  1270.6 10.0 slice-start.2
  1270.6 11.2 slice-start.3
Sparse Core Ops, SparseCore 0:
  236.1 108.1 reduce-scatter.28
  347.5 104.8 reduce-scatter.26
  455.7 104.9 reduce-scatter.24
  563.7 104.9 reduce-scatter.22
  672.3 104.9 reduce-scatter.20
  780.9 104.9 reduce-scatter.18
  936.5 101.5 all-gather.13
  1040.6 105.3 all-gather.11
  1148.6 105.3 all-gather.9
where the time goes:
time: 1310 us; the launch traced here: 1300 us
  waiting for transfers between devices  794 us (61%)
  matrix products  310 us (24%)
  other arithmetic  93.4 us (7%)
  local copies, waits for them, and re-layouts  40.1 us (3%)
  blocking collectives  39.3 us (3%)
  between operations  17.9 us (1%)
    unnamed x15, waiting for transfers between devices  488 us
    reshape x3, waiting for transfers between devices, step(): t.reshape(-1, *t.shape[2:])  305 us
    dot_general x5, matrix products, layer(): up = jnp.dot(a, w['w_up'], preferred_element_type=jnp.float32)  112 us
    dot_general x5, matrix products, layer(): gate = jnp.dot(a, w['w_gate'], preferred_element_type=jnp.float32)  106 us
    dot_general x5, matrix products, matmul(): jnp.dot(a, w, preferred_element_type=jnp.float32).astype(jnp.bfloat16)  91.8 us
    unnamed x4, other arithmetic  62.7 us
    unnamed x41, local copies, waits for them, and re-layouts  39.5 us
    reduce_sum x1, blocking collectives, of_a_group(): jnp.sum(g * g)  39.3 us
  transfers between devices with their start and end apart: 9, of which 8 were waited for; matrix products, arithmetic and copies ran while one was open for 13% of the time, Pallas kernels for 0%

commit v1 on v0

v1 whole, which is shorter than its diff:
```python
import functools
import math

import jax
import jax.numpy as jnp
from jax import lax
from jax.experimental import pallas as pl
from jax.experimental.pallas import tpu as pltpu
from jax.sharding import Mesh
from jax.sharding import PartitionSpec as P

F32, BF = jnp.float32, jnp.bfloat16
MESH = pl.DeviceIdType.MESH
MIB = 2**20
ANY = pl.BlockSpec(memory_space=pl.ANY)
DMA = pltpu.SemaphoreType.DMA
SIDE = 4


def dot(a, b):
    return jnp.dot(a, b, preferred_element_type=F32)


def dot_t(a, b):
    return lax.dot_general(a, b, (((1,), (1,)), ((), ())), preferred_element_type=F32)


def normed(h):
    wide = h.astype(F32)
    scale = lax.rsqrt(jnp.mean(wide * wide, -1, keepdims=True) + 1e-6)
    return (wide * scale).astype(BF)


def sigmoid(z):
    return 0.5 * jnp.tanh(0.5 * z) + 0.5


def ring(axis):
    me = lax.axis_index(axis)
    return me, lax.rem(me + 1, SIDE), lax.rem(me + SIDE - 1, SIDE)


def greet(peers):
    barrier = pltpu.get_barrier_semaphore()
    for axis, index in peers:
        pl.semaphore_signal(barrier, inc=1, device_id={axis: index}, device_id_type=MESH)
    pl.semaphore_wait(barrier, len(peers))


def remote(src, dst, send, recv, axis, index):
    return pltpu.make_async_remote_copy(
        src_ref=src, dst_ref=dst, send_sem=send, recv_sem=recv, device_id={axis: index}, device_id_type=MESH
    )


class Gather:
    def __init__(self, own, slots, send, recv):
        _, after, before = ring("x")
        half = own.shape[0] // 2
        top, bottom = pl.ds(0, half), pl.ds(half, half)
        c = lambda k, src, dst, to: remote(src, dst, send.at[k], recv.at[k], "x", to)
        self.first = [
            c(0, own.at[top], slots.at[0, top], after),
            c(1, own.at[bottom], slots.at[1, bottom], before),
            c(2, own.at[bottom], slots.at[0, bottom], after),
            c(3, own.at[top], slots.at[1, top], before),
        ]
        self.second = [
            c(4, slots.at[0, top], slots.at[2, top], after),
            c(5, slots.at[1, bottom], slots.at[2, bottom], before),
        ]

    def start(self):
        for copy in self.first:
            copy.start()

    def relay(self):
        for copy in self.first[:2]:
            copy.wait_recv()
        for copy in self.second:
            copy.start()

    def finish(self):
        for copy in self.first[2:] + self.second:
            copy.wait_recv()
        for copy in self.first + self.second:
            copy.wait_send()


def forward_kernel(steps, sub, x, dy, wg, wu, wd, h1, a1, a2, slots, acc, send, recv):
    j = pl.program_id(0)
    gather = Gather(dy, slots, send, recv)

    @pl.when(j == 0)
    def _():
        _, after, before = ring("x")
        greet([("x", after), ("x", before)])
        gather.start()
        a1[...] = normed(x[...])
        acc[...] = jnp.zeros_like(acc)

    @pl.when(j == steps // 2)
    def _():
        gather.relay()

    for i in range(x.shape[0] // sub):
        r = pl.ds(i * sub, sub)
        a = a1[r, :]
        gate, up = dot(a, wg[0]), dot(a, wu[0])
        acc[r, :] += dot((gate * sigmoid(gate) * up).astype(BF), wd[0])

    @pl.when(j == steps - 1)
    def _():
        h = x[...] + acc[...].astype(BF)
        h1[...] = h
        a2[...] = normed(h)
        gather.finish()


def own_kernel(steps, sub, h1, a2, dy, a2_any, a1_any, wg, wu, wd, dh1, slots, halves, accg, accu, send, recv, send1, recv1):
    j = pl.program_id(0)
    _, after, before = ring("x")
    gather = Gather(a2_any, slots, send, recv)
    half = a1_any.shape[0] // 2
    part = [
        remote(a1_any.at[pl.ds(0, half)], halves.at[0], send1.at[0], recv1.at[0], "x", after),
        remote(a1_any.at[pl.ds(half, half)], halves.at[1], send1.at[1], recv1.at[1], "x", before),
    ]

    @pl.when(j == 0)
    def _():
        greet([("x", after), ("x", before)])
        gather.start()
        accg[...] = jnp.zeros_like(accg)
        accu[...] = jnp.zeros_like(accu)

    @pl.when(j == steps // 3)
    def _():
        gather.relay()
        for copy in part:
            copy.start()

    for i in range(h1.shape[0] // sub):
        r = pl.ds(i * sub, sub)
        a, d = a2[r, :], dy[r, :]
        gate, up = dot(a, wg[0]), dot(a, wu[0])
        dhid = dot_t(d, wd[0]).astype(BF).astype(F32)
        s = sigmoid(gate)
        accu[r, :] += dot_t((dhid * (gate * s)).astype(BF), wu[0])
        accg[r, :] += dot_t((dhid * up * (s * (1.0 + gate * (1.0 - s)))).astype(BF), wg[0])

    @pl.when(j == steps - 1)
    def _():
        da = (accg[...].astype(BF).astype(F32) + accu[...].astype(BF).astype(F32)).astype(BF).astype(F32)
        wide = h1[...].astype(F32)
        scale = lax.rsqrt(jnp.mean(wide * wide, -1, keepdims=True) + 1e-6)
        along = jnp.sum(da * wide, -1, keepdims=True) * (scale * scale * scale * (1.0 / wide.shape[-1]))
        dh1[...] = dy[...] + (da * scale - wide * along).astype(BF)
        gather.finish()
        for copy in part:
            copy.wait()


def gate_row(xb, rows):
    return xb * (2 * rows) + lax.div(xb, 2) * (4 * rows)


def gradient_kernel(
    n, rows,
    a2, a2s, dy, dys, a1, a1h, dh1, wg, wu, wd,
    og, ou, od, osq, dslots, b1,
    A, D, AT, DT, hid, dg, du, ag, au, ad, dT, wbuf, far, raw, keep, own, summed, frecv, rm, rp, GT, XR,
    lsem, wsem, gsend, grecv, bsend, brecv, rsend, rrecv, xsend, xrecv,
):
    t = pl.program_id(0)
    last = 2 * n - 1
    x, xa, xb_ = ring("x")
    y, ya, yb = ring("y")
    T, Dm = a2.shape
    half = T // 2
    ft = wbuf.shape[2]
    chunk = ft // SIDE
    top, bottom = pl.ds(0, half), pl.ds(half, half)
    gather = Gather(dh1, dslots, gsend, grecv)
    bcopy = lambda k, src, to: remote(src, b1.at[k], bsend.at[k], brecv.at[k], "x", to)
    rest = [bcopy(0, a1.at[bottom], xa), bcopy(1, a1.at[top], xb_), bcopy(2, a1h.at[0], xa), bcopy(3, a1h.at[1], xb_)]

    def weights(t):
        layer, j, slot = 1 - lax.div(t, n), lax.rem(t, n), lax.rem(t, 2)
        out = []
        for k in range(SIDE):
            at = pl.multiple_of(x * (n * ft) + k * ft + j * chunk, chunk)
            to = pl.ds(k * chunk, chunk)
            out.append(pltpu.make_async_copy(wg.at[layer, :, pl.ds(at, chunk)], wbuf.at[slot, 0, :, to], wsem.at[slot, 3 * k]))
            out.append(pltpu.make_async_copy(wu.at[layer, :, pl.ds(at, chunk)], wbuf.at[slot, 1, :, to], wsem.at[slot, 3 * k + 1]))
            out.append(pltpu.make_async_copy(wd.at[layer, pl.ds(at, chunk), :], wbuf.at[slot, 2, to, :], wsem.at[slot, 3 * k + 2]))
        return out

    def load(pairs):
        copies = [pltpu.make_async_copy(src, dst, lsem.at[k]) for k, (src, dst) in enumerate(pairs)]
        for copy in copies:
            copy.start()
        for copy in copies:
            copy.wait()

    def transpose():
        def one(s, _):
            AT[s] = A[s].T
            DT[s] = D[s].T
            return 0

        lax.fori_loop(0, SIDE, one, 0)

    def reduction(t):
        s = lax.rem(t, 3)
        h = far.shape[1] // 2
        lo, hi = pl.ds(0, h), pl.ds(h, h)
        c = lambda k, src, dst, to: remote(src, dst, rsend.at[s, k], rrecv.at[s, k], "y", to)
        return [
            c(0, far.at[s, lo], frecv.at[s, lo], ya),
            c(1, far.at[s, hi], frecv.at[s, hi], yb),
            c(2, raw.at[s, hi], rm.at[s, hi], ya),
            c(3, raw.at[s, lo], rp.at[s, lo], yb),
            c(4, summed.at[s, lo], rm.at[s, lo], ya),
            c(5, summed.at[s, hi], rp.at[s, hi], yb),
        ]

    def pack(t):
        s = lax.rem(t, 3)
        dT[...] = ad[...].T

        def rows_for(rel):
            yd = lax.rem(y + rel, SIDE)
            parts = {}
            for b in range(SIDE):
                at = pl.multiple_of(b * (SIDE * rows) + yd * rows, rows)
                to = b * 2 * rows + (b // 2) * 4 * rows
                parts[to] = ag[pl.ds(at, rows), :]
                parts[to + rows] = au[pl.ds(at, rows), :]
            at = pl.multiple_of(yd * chunk, chunk)
            parts[4 * rows] = dT[pl.ds(at, chunk // 2), :]
            parts[6 * rows] = dT[pl.ds(at + chunk // 2, chunk // 2), :]
            return parts

        h = far.shape[1] // 2
        for to, v in rows_for(2).items():
            far[s, pl.ds(to, v.shape[0]), :] = v.astype(BF)
        for to, v in rows_for(1).items():
            if to < h:
                keep[s, pl.ds(to, v.shape[0]), :] = v
            else:
                raw[s, pl.ds(to, v.shape[0]), :] = v.astype(BF)
        for to, v in rows_for(3).items():
            if to < h:
                raw[s, pl.ds(to, v.shape[0]), :] = v.astype(BF)
            else:
                keep[s, pl.ds(to, v.shape[0]), :] = v
        for to, v in rows_for(0).items():
            own[s, pl.ds(to, v.shape[0]), :] = v

    def total(t):
        s = lax.rem(t, 3)
        copies = reduction(t)
        copies[0].wait_recv()
        copies[1].wait_recv()
        summed[s] = (keep[s] + frecv[s].astype(F32)).astype(BF)
        copies[4].start()
        copies[5].start()

    def across(t):
        out = []
        for r in range(1, SIDE):
            to = lax.rem(x + r, SIDE)
            at = pl.multiple_of(gate_row(to, rows), 2 * rows)
            out.append(remote(GT.at[t, pl.ds(at, 2 * rows)], XR.at[t, r - 1], xsend.at[t, r - 1], xrecv.at[t, r - 1], "x", to))
        return out

    def final(t):
        s = lax.rem(t, 3)
        copies = reduction(t)
        for copy in copies[2:]:
            copy.wait_recv()
        for copy in copies:
            copy.wait_send()
        GT[t] = (own[s] + rm[s].astype(F32) + rp[s].astype(F32)).astype(BF)
        for copy in across(t):
            copy.start()

    def assemble(t):
        layer, j = 1 - lax.div(t, n), lax.rem(t, n)
        for copy in across(t):
            copy.wait()
        squares = jnp.zeros((8, 128), F32)
        for r in range(SIDE):
            source = lax.rem(x + SIDE - r, SIDE)
            if r:
                piece = XR[t, r - 1]
            else:
                piece = GT[t, pl.ds(pl.multiple_of(gate_row(x, rows), 2 * rows), 2 * rows), :]
            wide = piece.astype(F32)
            squares += fold(wide * wide)
            for k in range(SIDE):
                at = pl.multiple_of(source * (n * ft) + k * ft + j * chunk, chunk)
                og[layer, :, pl.ds(at, chunk)] = piece[:rows, k * chunk : (k + 1) * chunk]
                ou[layer, :, pl.ds(at, chunk)] = piece[rows:, k * chunk : (k + 1) * chunk]
        piece = GT[t, 4 * rows : 8 * rows, :]
        wide = piece.astype(F32)
        squares += fold(wide * wide)
        od[layer, pl.ds(pl.multiple_of(j * chunk, chunk), chunk), :] = piece
        osq[...] += squares

    @pl.when(t == 0)
    def _():
        greet([("x", xa), ("x", xb_), ("x", lax.rem(x + 2, SIDE)), ("y", ya), ("y", yb)])
        gather.start()
        for copy in rest:
            copy.start()
        for copy in weights(t):
            copy.start()
        osq[...] = jnp.zeros_like(osq)
        load([(a2, A.at[0]), (dy, D.at[0])] + [(a2s.at[k], A.at[k + 1]) for k in range(3)] + [(dys.at[k], D.at[k + 1]) for k in range(3)])
        transpose()

    @pl.when(t == n)
    def _():
        gather.finish()
        for copy in rest:
            copy.wait()
        load(
            [(a1, A.at[0]), (dh1, D.at[0])]
            + [(a1h.at[0], A.at[1, top]), (b1.at[0], A.at[1, bottom]), (b1.at[1], A.at[2, top]), (a1h.at[1], A.at[2, bottom])]
            + [(b1.at[2], A.at[3, top]), (b1.at[3], A.at[3, bottom])]
            + [(dslots.at[k], D.at[k + 1]) for k in range(3)]
        )
        transpose()

    for copy in weights(t):
        copy.wait()

    @pl.when(t < last)
    def _():
        for copy in weights(t + 1):
            copy.start()

    slot = lax.rem(t, 2)
    sub = half
    ag[...] = jnp.zeros_like(ag)
    au[...] = jnp.zeros_like(au)
    ad[...] = jnp.zeros_like(ad)

    def chain(s, b):
        for i in range(T // sub):
            r = pl.ds(i * sub, sub)
            a, d = A[s, r, :], D[s, r, :]
            gate, up = dot(a, wbuf[slot, 0]), dot(a, wbuf[slot, 1])
            dhid = dot_t(d, wbuf[slot, 2]).astype(BF).astype(F32)
            g = sigmoid(gate)
            silu = gate * g
            hid[b, r, :] = (silu * up).astype(BF)
            du[b, r, :] = (dhid * silu).astype(BF)
            dg[b, r, :] = (dhid * up * (g * (1.0 + gate * (1.0 - g)))).astype(BF)

    def contract(s, b):
        ag[...] += dot(AT[s], dg[b])
        au[...] += dot(AT[s], du[b])
        ad[...] += dot(DT[s], hid[b])

    for s in range(SIDE):
        chain(s, s % 2)
        if s:
            contract(s - 1, (s - 1) % 2)
    contract(SIDE - 1, (SIDE - 1) % 2)

    @pl.when(t == 0)
    def _():
        gather.relay()

    @pl.when(t >= 3)
    def _():
        assemble(t - 3)

    @pl.when(t >= 2)
    def _():
        final(t - 2)

    @pl.when(t >= 1)
    def _():
        total(t - 1)

    pack(t)
    for copy in reduction(t)[:4]:
        copy.start()

    @pl.when(t == last)
    def _():
        final(t - 1)
        total(t)
        assemble(t - 2)
        assemble(t - 1)
        final(t)
        assemble(t)


def fold(v):
    out = None
    for i in range(v.shape[0] // 8):
        for k in range(v.shape[1] // 128):
            tile = v[i * 8 : i * 8 + 8, k * 128 : k * 128 + 128]
            out = tile if out is None else out + tile
    return out


def squares_kernel(mine, out, got, send, recv):
    x, y = lax.axis_index("x"), lax.axis_index("y")
    peers = [(lax.rem(x + i, SIDE), lax.rem(y + j, SIDE)) for i in range(SIDE) for j in range(SIDE)][1:]
    barrier = pltpu.get_barrier_semaphore()
    for px, py in peers:
        pl.semaphore_signal(barrier, inc=1, device_id={"x": px, "y": py}, device_id_type=MESH)
    pl.semaphore_wait(barrier, len(peers))
    copies = [
        pltpu.make_async_remote_copy(
            src_ref=mine, dst_ref=got.at[k], send_sem=send.at[k], recv_sem=recv.at[k], device_id={"x": px, "y": py}, device_id_type=MESH
        )
        for k, (px, py) in enumerate(peers)
    ]
    for copy in copies:
        copy.start()
    for copy in copies:
        copy.wait()
    total = mine[...]
    for k in range(len(peers)):
        total += got[k]
    out[...] = total


def update_kernel(count, _, sq, *refs):
    g, m, v, w, nw, nm, nv = (refs[3 * i : 3 * i + 3] for i in range(7))
    factor = jnp.minimum(1.0, 0.5 * lax.rsqrt(jnp.sum(sq[...]) / count + 1e-30))
    for i in range(3):
        grad = g[i][...].astype(F32) * factor
        new_m = 0.9 * m[i][...] + 0.1 * grad
        new_v = 0.95 * v[i][...] + 0.05 * grad * grad
        wide = w[i][...].astype(F32)
        step = new_m * lax.rsqrt(new_v + 1e-8) + 0.1 * wide
        nw[i][...] = (wide - 0.02 * step).astype(BF)
        nm[i][...] = new_m
        nv[i][...] = new_v


def gather_kernel(bg, bu, bd, og, ou, od, local, send, recv):
    x, xa, xb = ring("x")
    y, ya, yb = ring("y")
    greet([("x", xa), ("x", xb), ("y", ya), ("y", yb)])
    colours = [("x", xa, "y", ya, -1), ("x", xb, "y", yb, 1), ("y", ya, "x", xa, -1), ("y", yb, "x", xb, 1)]
    blocks, outs = (bg, bu, bd), (og, ou, od)

    def owner(colour, i, j):
        first, _, _, _, back = colours[colour]
        i, j = (i, j) if first == "x" else (j, i)
        return lax.rem(x + SIDE + back * i, SIDE) * SIDE + lax.rem(y + SIDE + back * j, SIDE)

    def place(piece, colour, d):
        rows = blocks[piece].shape[1]
        at = pl.multiple_of(d * rows, rows)
        if piece < 2:
            width = bg.shape[2] // 4
            return outs[piece].at[:, pl.ds(at, rows), pl.ds(colour * width, width)]
        return outs[piece].at[:, pl.ds(at + colour * (rows // 4), rows // 4), :]

    def source(piece, colour, i, j):
        if i or j:
            return place(piece, colour, owner(colour, i, j))
        if piece < 2:
            width = bg.shape[2] // 4
            return blocks[piece].at[:, :, pl.ds(colour * width, width)]
        rows = bd.shape[1] // 4
        return bd.at[:, pl.ds(colour * rows, rows), :]

    def hop(piece, colour, i, j, along):
        a, an, b, bn, _ = colours[colour]
        i2, j2 = (i + 1, j) if along == 0 else (i, j + 1)
        return remote(
            source(piece, colour, i, j), place(piece, colour, owner(colour, i, j)),
            send.at[piece, colour, along], recv.at[piece, colour, i2 * SIDE + j2], a if along == 0 else b, an if along == 0 else bn,
        )

    mine = x * SIDE + y
    locals_ = []
    for piece in range(3):
        rows = blocks[piece].shape[1]
        locals_.append(pltpu.make_async_copy(blocks[piece], outs[piece].at[:, pl.ds(pl.multiple_of(mine * rows, rows), rows), :], local.at[piece]))
    events = sorted((12 * p + 3 * i + 4 * j, p, i, j) for p in range(3) for i in range(SIDE) for j in range(SIDE))
    sent = []
    for _, p, i, j in events:
        for c in range(4):
            if i or j:
                hop(p, c, i - 1 if j == 0 else i, j - 1 if j else 0, 0 if j == 0 else 1).wait_recv()
            if j == 0 and i < SIDE - 1:
                copy = hop(p, c, i, j, 0)
                copy.start()
                sent.append(copy)
            if j < SIDE - 1:
                copy = hop(p, c, i, j, 1)
                copy.start()
                sent.append(copy)
        if (p, i, j) == (0, 0, 0):
            for copy in locals_:
                copy.start()
    for copy in sent:
        copy.wait_send()
    for copy in locals_:
        copy.wait()


def params(limit, collective=None):
    if collective is None:
        return pltpu.CompilerParams(vmem_limit_bytes=limit)
    return pltpu.CompilerParams(vmem_limit_bytes=limit, collective_id=collective, has_side_effects=True)


def step(x, dy, wg, wu, wd, mg, mu, md, vg, vu, vd):
    x, dy = x[0], dy[0]
    T, Dm = x.shape
    layers, _, ff = wg.shape
    state = jax.ShapeDtypeStruct((T, Dm), BF)
    slots = jax.ShapeDtypeStruct((3, T, Dm), BF)
    whole = pl.BlockSpec((T, Dm), lambda j: (0, 0))

    def weight_specs(layer, ft):
        return [
            pl.BlockSpec((1, Dm, ft), lambda j: (layer, 0, j)),
            pl.BlockSpec((1, Dm, ft), lambda j: (layer, 0, j)),
            pl.BlockSpec((1, ft, Dm), lambda j: (layer, j, 0)),
        ]

    ft, sub = 1024, 512
    h1, a1, a2, dys = pl.pallas_call(
        functools.partial(forward_kernel, ff // ft, sub),
        grid=(ff // ft,),
        in_specs=[whole, ANY, *weight_specs(0, ft)],
        out_specs=[whole] * 3 + [ANY],
        out_shape=[state] * 3 + [slots],
        scratch_shapes=[pltpu.VMEM((T, Dm), F32), DMA((6,)), DMA((6,))],
        compiler_params=params(60 * MIB, 0),
        name="forward",
    )(x, dy, wg, wu, wd)

    ft, sub = 1024, 1024
    dh1, a2s, a1h = pl.pallas_call(
        functools.partial(own_kernel, ff // ft, sub),
        grid=(ff // ft,),
        in_specs=[whole] * 3 + [ANY] * 2 + weight_specs(1, ft),
        out_specs=[whole, ANY, ANY],
        out_shape=[state, slots, jax.ShapeDtypeStruct((2, T // 2, Dm), BF)],
        scratch_shapes=[pltpu.VMEM((T, Dm), F32)] * 2 + [DMA((6,)), DMA((6,)), DMA((2,)), DMA((2,))],
        compiler_params=params(60 * MIB, 1),
        name="own",
    )(h1, a2, dy, a2, a1, wg, wu, wd)

    ft = 512
    n = ff // (SIDE * ft)
    rows = mg.shape[1]
    piece = 2 * SIDE * rows + ft // SIDE
    vm = pltpu.VMEM
    full = lambda *shape: pl.BlockSpec(shape, lambda t: (0,) * len(shape))
    gg, gu, gd, sq, _, _ = pl.pallas_call(
        functools.partial(gradient_kernel, n, rows),
        grid=(layers * n,),
        in_specs=[ANY] * 10,
        out_specs=[full(*mg.shape), full(*mu.shape), full(*md.shape), full(8, 128), ANY, ANY],
        out_shape=[jax.ShapeDtypeStruct(m.shape, BF) for m in (mg, mu, md)]
        + [jax.ShapeDtypeStruct((8, 128), F32), slots, jax.ShapeDtypeStruct((4, T // 2, Dm), BF)],
        scratch_shapes=[vm((SIDE, T, Dm), BF)] * 2
        + [vm((SIDE, Dm, T), BF)] * 2
        + [vm((2, T, ft), BF)] * 3
        + [vm((Dm, ft), F32)] * 4
        + [vm((2, 3, ft, Dm), BF)]
        + [vm((3, piece, ft), BF)] * 2
        + [vm((3, piece, ft), F32)] * 2
        + [vm((3, piece, ft), BF)] * 4
        + [vm((2 * n, piece, ft), BF), vm((2 * n, 3, 2 * rows, ft), BF)]
        + [DMA((12,)), DMA((2, 12)), DMA((6,)), DMA((6,)), DMA((4,)), DMA((4,)), DMA((3, 6)), DMA((3, 6)), DMA((2 * n, 3)), DMA((2 * n, 3))],
        compiler_params=params(63 * MIB, 2),
        name="gradients",
    )(a2, a2s, dy, dys, a1, a1h, dh1, wg, wu, wd)

    tiny = pl.BlockSpec(memory_space=pltpu.VMEM)
    peers = SIDE * SIDE - 1
    sq = pl.pallas_call(
        squares_kernel,
        in_specs=[tiny],
        out_specs=tiny,
        out_shape=jax.ShapeDtypeStruct((8, 128), F32),
        scratch_shapes=[vm((peers, 8, 128), F32), DMA((peers,)), DMA((peers,))],
        compiler_params=params(8 * MIB, 3),
        name="squares",
    )(sq)

    count = sum(w.size for w in (wg, wu, wd))
    me = (lax.axis_index("x") * SIDE + lax.axis_index("y")).astype(jnp.int32).reshape(1)
    parts = 4
    across = (1, rows, ff // parts)
    down = (1, md.shape[1] // parts, Dm)
    wide = [pl.BlockSpec(across, lambda l, c, me: (l, 0, c))] * 2
    tall = [pl.BlockSpec(down, lambda l, c, me: (l, c, 0))]
    blocks = wide + tall
    of_weights = [pl.BlockSpec(across, lambda l, c, me: (l, me[0], c))] * 2 + [pl.BlockSpec(down, lambda l, c, me: (l, me[0] * parts + c, 0))]
    shapes = lambda dt: [jax.ShapeDtypeStruct(m.shape, dt) for m in (mg, mu, md)]
    bg, bu, bd, *moments = pl.pallas_call(
        functools.partial(update_kernel, count),
        grid_spec=pltpu.PrefetchScalarGridSpec(
            num_scalar_prefetch=1,
            grid=(layers, parts),
            in_specs=[pl.BlockSpec((8, 128), lambda l, c, me: (0, 0)), *blocks, *blocks, *blocks, *of_weights],
            out_specs=[*blocks, *blocks, *blocks],
        ),
        out_shape=shapes(BF) + shapes(F32) + shapes(F32),
        compiler_params=params(48 * MIB),
        name="update",
    )(me, sq, gg, gu, gd, mg, mu, md, vg, vu, vd, wg, wu, wd)

    new = pl.pallas_call(
        gather_kernel,
        in_specs=[tiny] * 3,
        out_specs=[ANY] * 3,
        out_shape=[jax.ShapeDtypeStruct(w.shape, BF) for w in (wg, wu, wd)],
        scratch_shapes=[DMA((3,)), DMA((3, 4, 2)), DMA((3, 4, SIDE * SIDE))],
        compiler_params=params(16 * MIB, 4),
        name="gather",
    )(bg, bu, bd)

    return (*new, *moments)


def solution(mesh):
    side = math.isqrt(mesh.shape["dp"])
    torus = Mesh(mesh.devices.reshape(-1, side, side), ("rep", "x", "y"))
    batch = P(("rep", "x", "y"))
    rows = P(None, ("x", "y"))
    out_rows = P("rep", ("x", "y"))
    return jax.shard_map(
        step,
        mesh=torus,
        in_specs=(batch, batch, P(), P(), P(), *[rows] * 6),
        out_specs=(P("rep"),) * 3 + (out_rows,) * 6,
        check_vma=False,
    )
```

time: 1310 us -> 573 us (0.44); the launches traced: 1300 us -> 573 us
  waiting for transfers between devices: 794 us -> 0 us
  Pallas kernels: 0 us -> 545 us
  matrix products: 310 us -> 0 us
  other arithmetic: 93.4 us -> 0.01 us
  blocking collectives: 39.3 us -> 0 us
  between operations: 17.9 us -> 0.73 us
    pallas_call x0 -> x6, Pallas kernels: none -> 545 us  [the longest x1 253 us: step(): pl.pallas_call(gather_kernel, in_specs=[tiny] * 3, out_specs=[ANY] * 3, o...]
    unnamed x15 -> x0, waiting for transfers between devices: 488 us -> none
    dot_general x15 -> x0, matrix products: 310 us -> none  [the longest x5 112 us: layer(): up = jnp.dot(a, w['w_up'], preferred_element_type=jnp.float32)]
    reshape x3 -> x0, waiting for transfers between devices: 305 us -> none  [step(): t.reshape(-1, *t.shape[2:])]
    unnamed x4 -> x1, other arithmetic: 62.7 us -> 0.01 us
    reduce_sum x1 -> x0, blocking collectives: 39.3 us -> none  [of_a_group(): jnp.sum(g * g)]
    reshape x3 -> x0, other arithmetic: 18.1 us -> none  [step(): t.reshape(-1, *t.shape[2:])]
    unnamed x41 -> x17, local copies, waits for them, and re-layouts: 39.5 us -> 27.3 us
  transfers between devices with their start and end apart: 9 -> 0, of which waited for: 8 -> 0; matrix products, arithmetic and copies ran while one was open for 13% -> 0% of each run, Pallas kernels for 0% -> 0%
where the time goes in v1:
time: 573 us
  Pallas kernels  545 us (95%)
  local copies, waits for them, and re-layouts  27.3 us (5%)
    pallas_call x1, Pallas kernels, step(): pl.pallas_call(gather_kernel, in_specs=[tiny] * 3, out_specs=[ANY] * 3, o...  253 us
    pallas_call x1, Pallas kernels, step(): pl.pallas_call(functools.partial(gradient_kernel, n, rows), grid=(layers...  170 us
    pallas_call x1, Pallas kernels, step(): pl.pallas_call(functools.partial(own_kernel, ff // ft, sub), grid=(ff //...  56.6 us
    pallas_call x1, Pallas kernels, step(): pl.pallas_call(functools.partial(forward_kernel, ff // ft, sub), grid=(ff...  42.2 us
    unnamed x17, local copies, waits for them, and re-layouts  27.3 us
    pallas_call x1, Pallas kernels, step(): pl.pallas_call(functools.partial(update_kernel, count), grid_spec=pltpu.P...  14.6 us

profile of v1, /device:TPU:96, one launch (start us, length us, event | category | flops | bytes accessed | tf_op | source)
XLA Modules:
  0.0 572.8 jit_solution(10015907967545632884)
XLA Ops:
  0.6 42.2 %forward.1 = (bf16[1024,512]{1,0:T(8,128)(2,1)}, bf16[1024,512]{1,0:T(8,128)(2,1)}, bf16[1024,512]{1,0:T(8,128)(2,1)}, bf16[3,1024,512]{2,1,0:T(8,128)(2,1)}) custom-call(bf16[1024,512]{1,0:T(8,128)(2,1)} %bitcast.8, bf16[1024,512]{1,0:T(8,128)(2,1)} %bitcast.5, bf16[2,512,8192]{2,1,0:T(8,128)(2,1)} %refs_9_.1, bf16[2,512,8192]{2,1,0:T(8,128)(2,1)} %refs_10_.1, ...), custom_call_target="tpu_custom_call" | custom-call | tf_op jit(solution)/shard_map/forward/pallas_call | solution.py:537
  42.9 56.6 %own.1 = (bf16[1024,512]{1,0:T(8,128)(2,1)}, bf16[3,1024,512]{2,1,0:T(8,128)(2,1)}, bf16[2,512,512]{2,1,0:T(8,128)(2,1)}) custom-call(bf16[1024,512]{1,0:T(8,128)(2,1)} %get-tuple-element.33.h1, bf16[1024,512]{1,0:T(8,128)(2,1)} %get-tuple-element.32.a2.a2_any, bf16[1024,512]{1,0:T(8,128)(2,1)} %bitcast.6, bf16[1024,512]{1,0:T(8,128)(2,1)} %get-tuple-element.32.a2.a2_any, ...), custom_call_target="tpu_custom_call" | custom-call | tf_op jit(solution)/shard_map/own/pallas_call | solution.py:549
  99.5 170.4 %gradients.1 = (bf16[2,32,8192]{2,1,0:T(8,128)(2,1)}, bf16[2,32,8192]{2,1,0:T(8,128)(2,1)}, bf16[2,512,512]{2,1,0:T(8,128)(2,1)}, f32[8,128]{1,0:T(8,128)}, bf16...) custom-call(bf16[1024,512]{1,0:T(8,128)(2,1)} %get-tuple-element.32.a2.a2_any, ...), custom_call_target="tpu_custom_call" | custom-call | tf_op jit(solution)/shard_map/gradients/pallas_call | solution.py:566
  269.9 0.0 copy-start.2
  269.9 0.7 copy-done.2
  270.6 8.1 %squares.1.sq = f32[8,128]{1,0:T(8,128)S(1)} custom-call(f32[8,128]{1,0:T(8,128)S(1)} %copy-done.2), custom_call_target="tpu_custom_call" | custom-call | tf_op jit(solution)/shard_map/squares/pallas_call | solution.py:589
  278.7 0.0 copy-start
  278.7 1.2 copy-done
  279.9 0.0 copy-start.1
  279.9 1.2 copy-done.1
  281.1 14.6 %update.1 = (bf16[2,32,8192]{2,1,0:T(8,128)(2,1)S(1)}, bf16[2,32,8192]{2,1,0:T(8,128)(2,1)S(1)}, bf16[2,512,512]{2,1,0:T(8,128)(2,1)S(1)}, f32[2,32,8192]{2,1,0:...) custom-call(s32[1]{0:T(128)} %bitcast._, ...), custom_call_target="tpu_custom_call" | custom-call | tf_op jit(solution)/shard_map/update/pallas_call | solution.py:609
  295.7 252.8 %gather.1 = (bf16[2,512,8192]{2,1,0:T(8,128)(2,1)S(1)}, bf16[2,512,8192]{2,1,0:T(8,128)(2,1)S(1)}, bf16[2,8192,512]{2,1,0:T(8,128)(2,1)}) custom-call(bf16[2,32,8192]{2,1,0:T(8,128)(2,1)S(1)} %get-tuple-element.43.bg, bf16[2,32,8192]{2,1,0:T(8,128)(2,1)S(1)} %get-tuple-element.44.bu, bf16[2,512,512]{2,1,0:T(8,128)(2,1)S(1)} %get-tuple-element.45.bd), custom_call_target="tpu_custom_call" | custom-call | tf_op jit(solution)/shard_map/gather/pallas_call | solution.py:622
  548.5 0.0 slice-start
  548.6 0.0 slice-start.1
  548.6 8.5 %copy.23 = bf16[2,512,8192]{2,1,0:T(8,128)(2,1)} copy(bf16[2,512,8192]{2,1,0:T(8,128)(2,1)S(1)} %get-tuple-element.64) | data formatting | bytes 33554432
  557.1 0.0 slice-start.2
  557.1 0.0 slice-start.3
  557.1 8.4 %copy.24 = bf16[2,512,8192]{2,1,0:T(8,128)(2,1)} copy(bf16[2,512,8192]{2,1,0:T(8,128)(2,1)S(1)} %get-tuple-element.65) | data formatting | bytes 33554432
  565.5 0.0 slice-done
  565.5 0.0 slice-done.1
  565.5 0.0 slice-done.2
  565.5 1.1 slice-done.3
  566.6 6.2 %copy.25 = bf16[2,8192,512]{2,1,0:T(8,128)(2,1)} copy(bf16[2,8192,512]{2,1,0:T(8,128)(2,1)S(1)} %bitcast.4) | data formatting | bytes 33554432
  (1 shorter events, 0.0 us)
Async XLA Ops:
  269.9 0.7 copy-start.2
  278.7 1.2 copy-start
  279.9 1.2 copy-start.1
  548.5 17.0 %slice-start = ((s8[16777216]{0:T(1024)(128)(4,1)}), s8[4194304]{0:T(1024)(128)(4,1)S(1)}, s32[]{:S(2)}) async-start(s8[16777216]{0:T(1024)(128)(4,1)} %bitcast.3), calls=%async_computation | async-start | bytes 8388608
  548.6 16.9 %slice-start.1 = ((s8[16777216]{0:T(1024)(128)(4,1)}), s8[4194304]{0:T(1024)(128)(4,1)S(1)}, s32[]{:S(2)}) async-start(s8[16777216]{0:T(1024)(128)(4,1)} %bitcast.3), calls=%async_computation.1 | async-start | bytes 8388608
  557.1 8.4 %slice-start.2 = ((s8[16777216]{0:T(1024)(128)(4,1)}), s8[4194304]{0:T(1024)(128)(4,1)S(1)}, s32[]{:S(2)}) async-start(s8[16777216]{0:T(1024)(128)(4,1)} %bitcast.3), calls=%async_computation.2 | async-start | bytes 8388608
  557.1 9.5 %slice-start.3 = ((s8[16777216]{0:T(1024)(128)(4,1)}), s8[4194304]{0:T(1024)(128)(4,1)S(1)}, s32[]{:S(2)}) async-start(s8[16777216]{0:T(1024)(128)(4,1)} %bitcast.3), calls=%async_computation.3 | async-start | bytes 8388608

commit v2 on v1

v2 whole, which is shorter than its diff:
```python
import functools
import math

import jax
import jax.numpy as jnp
from jax import lax
from jax.experimental import pallas as pl
from jax.experimental.pallas import tpu as pltpu
from jax.sharding import Mesh
from jax.sharding import PartitionSpec as P

F32, BF = jnp.float32, jnp.bfloat16
MESH = pl.DeviceIdType.MESH
MIB = 2**20
ANY = pl.BlockSpec(memory_space=pl.ANY)
DMA = pltpu.SemaphoreType.DMA
SIDE = 4


def dot(a, b):
    return jnp.dot(a, b, preferred_element_type=F32)


def dot_t(a, b):
    return lax.dot_general(a, b, (((1,), (1,)), ((), ())), preferred_element_type=F32)


def normed(h):
    wide = h.astype(F32)
    scale = lax.rsqrt(jnp.mean(wide * wide, -1, keepdims=True) + 1e-6)
    return (wide * scale).astype(BF)


def sigmoid(z):
    return 0.5 * jnp.tanh(0.5 * z) + 0.5


def ring(axis):
    me = lax.axis_index(axis)
    return me, lax.rem(me + 1, SIDE), lax.rem(me + SIDE - 1, SIDE)


def greet(peers):
    barrier = pltpu.get_barrier_semaphore()
    for axis, index in peers:
        pl.semaphore_signal(barrier, inc=1, device_id={axis: index}, device_id_type=MESH)
    pl.semaphore_wait(barrier, len(peers))


def remote(src, dst, send, recv, axis, index):
    return pltpu.make_async_remote_copy(
        src_ref=src, dst_ref=dst, send_sem=send, recv_sem=recv, device_id={axis: index}, device_id_type=MESH
    )


class Gather:
    def __init__(self, own, slots, send, recv):
        _, after, before = ring("x")
        half = own.shape[0] // 2
        top, bottom = pl.ds(0, half), pl.ds(half, half)
        c = lambda k, src, dst, to: remote(src, dst, send.at[k], recv.at[k], "x", to)
        self.first = [
            c(0, own.at[top], slots.at[0, top], after),
            c(1, own.at[bottom], slots.at[1, bottom], before),
            c(2, own.at[bottom], slots.at[0, bottom], after),
            c(3, own.at[top], slots.at[1, top], before),
        ]
        self.second = [
            c(4, slots.at[0, top], slots.at[2, top], after),
            c(5, slots.at[1, bottom], slots.at[2, bottom], before),
        ]

    def start(self):
        for copy in self.first:
            copy.start()

    def relay(self):
        for copy in self.first[:2]:
            copy.wait_recv()
        for copy in self.second:
            copy.start()

    def finish(self):
        for copy in self.first[2:] + self.second:
            copy.wait_recv()
        for copy in self.first + self.second:
            copy.wait_send()


def chain_kernel(
    steps, x, dy, dy_any, wg, wu, wd, a1, a2, dh1, dys, a2s, halves, h1, accg, accu, send, recv, send2, recv2, send1, recv1
):
    j = pl.program_id(0)
    _, after, before = ring("x")
    half = a1.shape[0] // 2
    gather_dy = Gather(dy_any, dys, send, recv)
    gather_a2 = Gather(a2, a2s, send2, recv2)
    part = [
        remote(a1.at[pl.ds(0, half)], halves.at[0], send1.at[0], recv1.at[0], "x", after),
        remote(a1.at[pl.ds(half, half)], halves.at[1], send1.at[1], recv1.at[1], "x", before),
    ]
    tiles = [pl.ds(k, 256) for k in range(0, wg.shape[2], 256)]

    @pl.when(j == 0)
    def _():
        greet([("x", after), ("x", before)])
        gather_dy.start()
        a1[...] = normed(x[...])
        accg[...] = jnp.zeros_like(accg)

    @pl.when(j == steps // 2)
    def _():
        gather_dy.relay()

    @pl.when(j == steps)
    def _():
        gather_a2.start()
        accg[...] = jnp.zeros_like(accg)
        accu[...] = jnp.zeros_like(accu)

    @pl.when(j == steps + 3)
    def _():
        gather_dy.finish()
        gather_a2.relay()
        for copy in part:
            copy.start()

    @pl.when(j < steps)
    def _():
        a = a1[...]
        hidden = []
        for k in tiles:
            gate, up = dot(a, wg[0, :, k]), dot(a, wu[0, :, k])
            hidden.append((gate * sigmoid(gate) * up).astype(BF))
        accg[...] += dot(jnp.concatenate(hidden, 1), wd[0])

    @pl.when(j == steps - 1)
    def _():
        h = x[...] + accg[...].astype(BF)
        h1[...] = h
        a2[...] = normed(h)

    @pl.when(j >= steps)
    def _():
        a, d = a2[...], dy[...]
        by_up, by_gate = [], []
        for k in tiles:
            gate, up = dot(a, wg[0, :, k]), dot(a, wu[0, :, k])
            dhid = dot_t(d, wd[0, k, :]).astype(BF).astype(F32)
            s = sigmoid(gate)
            silu = gate * s
            by_up.append((dhid * silu).astype(BF))
            by_gate.append((dhid * up * (s + silu * (1.0 - s))).astype(BF))
        accu[...] += dot_t(jnp.concatenate(by_up, 1), wu[0])
        accg[...] += dot_t(jnp.concatenate(by_gate, 1), wg[0])

    @pl.when(j == 2 * steps - 1)
    def _():
        da = (accg[...].astype(BF).astype(F32) + accu[...].astype(BF).astype(F32)).astype(BF).astype(F32)
        wide = h1[...].astype(F32)
        scale = lax.rsqrt(jnp.mean(wide * wide, -1, keepdims=True) + 1e-6)
        along = jnp.sum(da * wide, -1, keepdims=True) * (scale * scale * scale * (1.0 / wide.shape[-1]))
        dh1[...] = dy[...] + (da * scale - wide * along).astype(BF)
        gather_a2.finish()
        for copy in part:
            copy.wait()


def gate_row(xb, rows):
    return xb * (2 * rows) + lax.div(xb, 2) * (4 * rows)


def gradient_kernel(
    n, rows,
    a2, a2s, dy, dys, a1, a1h, dh1, wg, wu, wd,
    og, ou, od, osq, dslots, b1,
    A, D, AT, DT, hid, dg, du, silus, slopes, ag, au, ad, dT, wbuf, far, raw, keep, own, summed, frecv, rm, rp, GT, XR, others,
    lsem, wsem, gsend, grecv, bsend, brecv, rsend, rrecv, xsend, xrecv, qsend, qrecv,
):
    t = pl.program_id(0)
    last = 2 * n - 1
    x, xa, xb_ = ring("x")
    y, ya, yb = ring("y")
    T, Dm = a2.shape
    half = T // 2
    ft = wbuf.shape[2]
    chunk = ft // SIDE
    top, bottom = pl.ds(0, half), pl.ds(half, half)
    gather = Gather(dh1, dslots, gsend, grecv)
    bcopy = lambda k, src, to: remote(src, b1.at[k], bsend.at[k], brecv.at[k], "x", to)
    rest = [bcopy(0, a1.at[bottom], xa), bcopy(1, a1.at[top], xb_), bcopy(2, a1h.at[0], xa), bcopy(3, a1h.at[1], xb_)]

    def weights(t):
        layer, j, slot = 1 - lax.div(t, n), lax.rem(t, n), lax.rem(t, 2)
        out = []
        for k in range(SIDE):
            at = pl.multiple_of(x * (n * ft) + k * ft + j * chunk, chunk)
            to = pl.ds(k * chunk, chunk)
            out.append(pltpu.make_async_copy(wg.at[layer, :, pl.ds(at, chunk)], wbuf.at[slot, 0, :, to], wsem.at[slot, 3 * k]))
            out.append(pltpu.make_async_copy(wu.at[layer, :, pl.ds(at, chunk)], wbuf.at[slot, 1, :, to], wsem.at[slot, 3 * k + 1]))
            out.append(pltpu.make_async_copy(wd.at[layer, pl.ds(at, chunk), :], wbuf.at[slot, 2, to, :], wsem.at[slot, 3 * k + 2]))
        return out

    def loads(pairs):
        return [pltpu.make_async_copy(src, dst, lsem.at[k]) for k, (src, dst) in enumerate(pairs)]

    first = lambda: loads([(a2, A.at[0]), (dy, D.at[0])] + [(a2s.at[k], A.at[k + 1]) for k in range(3)] + [(dys.at[k], D.at[k + 1]) for k in range(3)])
    second = lambda: loads(
        [(a1, A.at[0]), (dh1, D.at[0])]
        + [(a1h.at[0], A.at[1, top]), (b1.at[0], A.at[1, bottom]), (b1.at[1], A.at[2, top]), (a1h.at[1], A.at[2, bottom])]
        + [(b1.at[2], A.at[3, top]), (b1.at[3], A.at[3, bottom])]
        + [(dslots.at[k], D.at[k + 1]) for k in range(3)]
    )

    def reduction(t):
        s = lax.rem(t, 3)
        h = far.shape[1] // 2
        lo, hi = pl.ds(0, h), pl.ds(h, h)
        c = lambda k, src, dst, to: remote(src, dst, rsend.at[s, k], rrecv.at[s, k], "y", to)
        return [
            c(0, far.at[s, lo], frecv.at[s, lo], ya),
            c(1, far.at[s, hi], frecv.at[s, hi], yb),
            c(2, raw.at[s, hi], rm.at[s, hi], ya),
            c(3, raw.at[s, lo], rp.at[s, lo], yb),
            c(4, summed.at[s, lo], rm.at[s, lo], ya),
            c(5, summed.at[s, hi], rp.at[s, hi], yb),
        ]

    def pack(t):
        s = lax.rem(t, 3)
        dT[...] = ad[...].T

        def rows_for(rel):
            yd = lax.rem(y + rel, SIDE)
            parts = {}
            for b in range(SIDE):
                at = pl.multiple_of(b * (SIDE * rows) + yd * rows, rows)
                to = b * 2 * rows + (b // 2) * 4 * rows
                parts[to] = ag[pl.ds(at, rows), :]
                parts[to + rows] = au[pl.ds(at, rows), :]
            at = pl.multiple_of(yd * chunk, chunk)
            parts[4 * rows] = dT[pl.ds(at, chunk // 2), :]
            parts[6 * rows] = dT[pl.ds(at + chunk // 2, chunk // 2), :]
            return parts

        h = far.shape[1] // 2
        for to, v in rows_for(2).items():
            far[s, pl.ds(to, v.shape[0]), :] = v.astype(BF)
        for to, v in rows_for(1).items():
            if to < h:
                keep[s, pl.ds(to, v.shape[0]), :] = v
            else:
                raw[s, pl.ds(to, v.shape[0]), :] = v.astype(BF)
        for to, v in rows_for(3).items():
            if to < h:
                raw[s, pl.ds(to, v.shape[0]), :] = v.astype(BF)
            else:
                keep[s, pl.ds(to, v.shape[0]), :] = v
        for to, v in rows_for(0).items():
            own[s, pl.ds(to, v.shape[0]), :] = v

    def total(t):
        s = lax.rem(t, 3)
        copies = reduction(t)
        copies[0].wait_recv()
        copies[1].wait_recv()
        summed[s] = (keep[s] + frecv[s].astype(F32)).astype(BF)
        copies[4].start()
        copies[5].start()

    def across(t):
        out, g = [], lax.rem(t, 4)
        for r in range(1, SIDE):
            to = lax.rem(x + r, SIDE)
            at = pl.multiple_of(gate_row(to, rows), 2 * rows)
            out.append(remote(GT.at[g, pl.ds(at, 2 * rows)], XR.at[g, r - 1], xsend.at[g, r - 1], xrecv.at[g, r - 1], "x", to))
        return out

    def final(t):
        s, g = lax.rem(t, 3), lax.rem(t, 4)
        copies = reduction(t)
        for copy in copies[2:]:
            copy.wait_recv()
        for copy in copies:
            copy.wait_send()
        mine = (own[s] + rm[s].astype(F32) + rp[s].astype(F32)).astype(BF)
        GT[g] = mine
        for copy in across(t):
            copy.start()
        wide = mine.astype(F32)
        osq[...] += fold(wide * wide)

    def assemble(t):
        layer, j, g = 1 - lax.div(t, n), lax.rem(t, n), lax.rem(t, 4)
        for copy in across(t):
            copy.wait()
        for r in range(SIDE):
            source = lax.rem(x + SIDE - r, SIDE)
            if r:
                piece = XR[g, r - 1]
            else:
                piece = GT[g, pl.ds(pl.multiple_of(gate_row(x, rows), 2 * rows), 2 * rows), :]
            for k in range(SIDE):
                at = pl.multiple_of(source * (n * ft) + k * ft + j * chunk, chunk)
                og[layer, :, pl.ds(at, chunk)] = piece[:rows, k * chunk : (k + 1) * chunk]
                ou[layer, :, pl.ds(at, chunk)] = piece[rows:, k * chunk : (k + 1) * chunk]
        od[layer, pl.ds(pl.multiple_of(j * chunk, chunk), chunk), :] = GT[g, 4 * rows : 8 * rows, :]

    peers = [(lax.rem(x + i, SIDE), lax.rem(y + k, SIDE)) for i in range(SIDE) for k in range(SIDE)][1:]

    @pl.when(t == 0)
    def _():
        for copy in first() + weights(t):
            copy.start()
        barrier = pltpu.get_barrier_semaphore()
        for px, py in peers:
            pl.semaphore_signal(barrier, inc=1, device_id={"x": px, "y": py}, device_id_type=MESH)
        pl.semaphore_wait(barrier, len(peers))
        gather.start()
        for copy in rest:
            copy.start()
        osq[...] = jnp.zeros_like(osq)
        for copy in first():
            copy.wait()

    @pl.when(t == n)
    def _():
        for copy in second():
            copy.wait()

    for copy in weights(t):
        copy.wait()

    @pl.when(t < last)
    def _():
        for copy in weights(t + 1):
            copy.start()

    slot = lax.rem(t, 2)
    sub = silus.shape[1]
    ag[...] = jnp.zeros_like(ag)
    au[...] = jnp.zeros_like(au)
    ad[...] = jnp.zeros_like(ad)

    def chain(s, b):
        AT[b] = A[s].T
        DT[b] = D[s].T
        for i in range(T // sub):
            r = pl.ds(i * sub, sub)
            a, d = A[s, r, :], D[s, r, :]
            for k in range(0, ft, 256):
                k = pl.ds(k, 256)
                gate = dot(a, wbuf[slot, 0, :, k])
                g = sigmoid(gate)
                silu = gate * g
                silus[b, :, k] = silu
                slopes[b, :, k] = g + silu * (1.0 - g)
                dhid = dot_t(d, wbuf[slot, 2, k, :]).astype(BF).astype(F32)
                du[b, r, k] = (dhid * silus[b, :, k]).astype(BF)
                slopes[b, :, k] = slopes[b, :, k] * dhid
                up = dot(a, wbuf[slot, 1, :, k])
                hid[b, r, k] = (silus[b, :, k] * up).astype(BF)
                dg[b, r, k] = (slopes[b, :, k] * up).astype(BF)

    def contract(b):
        ag[...] += dot(AT[b], dg[b])
        au[...] += dot(AT[b], du[b])
        ad[...] += dot(DT[b], hid[b])

    for s in range(SIDE):
        chain(s, s % 2)
        if s:
            contract((s - 1) % 2)
        if s == 1:
            pl.when(t >= 1)(functools.partial(total, t - 1))
    contract((SIDE - 1) % 2)

    @pl.when(t == n - 1)
    def _():
        gather.finish()
        for copy in rest:
            copy.wait()
        for copy in second():
            copy.start()

    @pl.when(t == 0)
    def _():
        gather.relay()

    @pl.when(t >= 3)
    def _():
        assemble(t - 3)

    @pl.when(t >= 2)
    def _():
        final(t - 2)

    pack(t)
    for copy in reduction(t)[:4]:
        copy.start()

    @pl.when(t == last)
    def _():
        final(t - 1)
        total(t)
        assemble(t - 2)
        final(t)
        copies = [
            pltpu.make_async_remote_copy(
                src_ref=osq, dst_ref=others.at[k], send_sem=qsend.at[k], recv_sem=qrecv.at[k], device_id={"x": px, "y": py}, device_id_type=MESH
            )
            for k, (px, py) in enumerate(peers)
        ]
        for copy in copies:
            copy.start()
        assemble(t - 1)
        assemble(t)
        for copy in copies:
            copy.wait()
        total_squares = osq[...]
        for k in range(len(peers)):
            total_squares += others[k]
        osq[...] = total_squares


def fold(v):
    out = None
    for i in range(v.shape[0] // 8):
        for k in range(v.shape[1] // 128):
            tile = v[i * 8 : i * 8 + 8, k * 128 : k * 128 + 128]
            out = tile if out is None else out + tile
    return out


def update_kernel(count, parts, sq, *refs):
    g, m, v, w, nw, nm, nv, bm, bv, bw = (refs[3 * i : 3 * i + 3] for i in range(10))
    came, left = refs[30:]
    mine = lax.axis_index("x") * SIDE + lax.axis_index("y")
    pieces = [(i, l, c) for i in range(3) for l in range(g[0].shape[0]) for c in range(parts)]

    def at(i, l, c, first=0):
        _, rows, width = g[i].shape
        if i < 2:
            return (l, pl.ds(first, rows), pl.ds(c * (width // parts), width // parts))
        return (l, pl.ds(first + c * (rows // parts), rows // parts), slice(None))

    def arrivals(k):
        i, l, c = pieces[k]
        here = at(i, l, c)
        there = at(i, l, c, pl.multiple_of(mine * g[i].shape[1], g[i].shape[1]))
        return [
            pltpu.make_async_copy(m[i].at[here], bm[i].at[here], came.at[k, 0]),
            pltpu.make_async_copy(v[i].at[here], bv[i].at[here], came.at[k, 1]),
            pltpu.make_async_copy(w[i].at[there], bw[i].at[here], came.at[k, 2]),
        ]

    def departures(k):
        i, l, c = pieces[k]
        here = at(i, l, c)
        return [
            pltpu.make_async_copy(bm[i].at[here], nm[i].at[here], left.at[k, 0]),
            pltpu.make_async_copy(bv[i].at[here], nv[i].at[here], left.at[k, 1]),
        ]

    for k in range(len(pieces)):
        for copy in arrivals(k):
            copy.start()
    factor = jnp.minimum(1.0, 0.5 * lax.rsqrt(jnp.sum(sq[...], keepdims=True) / count + 1e-30))
    for k, (i, l, c) in enumerate(pieces):
        here = at(i, l, c)
        for copy in arrivals(k):
            copy.wait()
        grad = g[i][here].astype(F32) * factor
        new_m = 0.9 * bm[i][here] + 0.1 * grad
        new_v = 0.95 * bv[i][here] + 0.05 * grad * grad
        wide = bw[i][here].astype(F32)
        step = new_m * lax.rsqrt(new_v + 1e-8) + 0.1 * wide
        nw[i][here] = (wide - 0.02 * step).astype(BF)
        bm[i][here] = new_m
        bv[i][here] = new_v
        for copy in departures(k):
            copy.start()
    for k in range(len(pieces)):
        for copy in departures(k):
            copy.wait()


def gather_kernel(bg, bu, bd, og, ou, od, local, send, recv):
    x, xa, xb = ring("x")
    y, ya, yb = ring("y")
    greet([("x", xa), ("x", xb), ("y", ya), ("y", yb)])
    colours = [("x", xa, "y", ya, -1), ("x", xb, "y", yb, 1), ("y", ya, "x", xa, -1), ("y", yb, "x", xb, 1)]
    blocks, outs = (bg, bu, bd), (og, ou, od)

    def owner(colour, i, j):
        first, _, _, _, back = colours[colour]
        i, j = (i, j) if first == "x" else (j, i)
        return lax.rem(x + SIDE + back * i, SIDE) * SIDE + lax.rem(y + SIDE + back * j, SIDE)

    def place(piece, colour, d):
        rows = blocks[piece].shape[1]
        at = pl.multiple_of(d * rows, rows)
        if piece < 2:
            width = bg.shape[2] // 4
            return outs[piece].at[:, pl.ds(at, rows), pl.ds(colour * width, width)]
        return outs[piece].at[:, pl.ds(at + colour * (rows // 4), rows // 4), :]

    def source(piece, colour, i, j):
        if i or j:
            return place(piece, colour, owner(colour, i, j))
        if piece < 2:
            width = bg.shape[2] // 4
            return blocks[piece].at[:, :, pl.ds(colour * width, width)]
        rows = bd.shape[1] // 4
        return bd.at[:, pl.ds(colour * rows, rows), :]

    def hop(piece, colour, i, j, along):
        a, an, b, bn, _ = colours[colour]
        i2, j2 = (i + 1, j) if along == 0 else (i, j + 1)
        return remote(
            source(piece, colour, i, j), place(piece, colour, owner(colour, i, j)),
            send.at[piece, colour, along], recv.at[piece, colour, i2 * SIDE + j2], a if along == 0 else b, an if along == 0 else bn,
        )

    mine = x * SIDE + y
    locals_ = []
    for piece in range(3):
        rows = blocks[piece].shape[1]
        locals_.append(pltpu.make_async_copy(blocks[piece], outs[piece].at[:, pl.ds(pl.multiple_of(mine * rows, rows), rows), :], local.at[piece]))
    events = sorted((12 * p + 3 * i + 4 * j, p, i, j) for p in range(3) for i in range(SIDE) for j in range(SIDE))
    sent = []
    for _, p, i, j in events:
        for c in range(4):
            if i or j:
                hop(p, c, i - 1 if j == 0 else i, j - 1 if j else 0, 0 if j == 0 else 1).wait_recv()
            if j == 0 and i < SIDE - 1:
                copy = hop(p, c, i, j, 0)
                copy.start()
                sent.append(copy)
            if j < SIDE - 1:
                copy = hop(p, c, i, j, 1)
                copy.start()
                sent.append(copy)
        if (p, i, j) == (0, 0, 0):
            for copy in locals_:
                copy.start()
    for copy in sent:
        copy.wait_send()
    for copy in locals_:
        copy.wait()


def out_kernel(src, dst, sem):
    part = src.shape[1] // 4
    copies = []
    for k in range(2 * 4):
        at = (k // 4, pl.ds(k % 4 * part, part))
        copies.append(pltpu.make_async_copy(src.at[at], dst.at[at], sem.at[k]))
    for copy in copies:
        copy.start()
    for copy in copies:
        copy.wait()


def cost(units, w):
    return pl.CostEstimate(flops=units * 2 * 1024 * w.shape[1] * w.shape[2], bytes_accessed=4 * w.size, transcendentals=0)


def params(limit, collective=None):
    if collective is None:
        return pltpu.CompilerParams(vmem_limit_bytes=limit)
    return pltpu.CompilerParams(vmem_limit_bytes=limit, collective_id=collective, has_side_effects=True)


def step(x, dy, wg, wu, wd, mg, mu, md, vg, vu, vd):
    x, dy = x[0], dy[0]
    T, Dm = x.shape
    layers, _, ff = wg.shape
    state = jax.ShapeDtypeStruct((T, Dm), BF)
    slots = jax.ShapeDtypeStruct((3, T, Dm), BF)
    whole = pl.BlockSpec((T, Dm), lambda j: (0, 0))

    tiny = pl.BlockSpec(memory_space=pltpu.VMEM)
    ft = 1024
    steps = ff // ft
    across = pl.BlockSpec((1, Dm, ft), lambda j: (lax.div(j, steps), 0, lax.rem(j, steps)))
    down = pl.BlockSpec((1, ft, Dm), lambda j: (lax.div(j, steps), lax.rem(j, steps), 0))
    a1, a2, dh1, dys, a2s, a1h = pl.pallas_call(
        functools.partial(chain_kernel, steps),
        grid=(layers * steps,),
        in_specs=[whole, whole, ANY, across, across, down],
        out_specs=[whole] * 3 + [ANY] * 3,
        out_shape=[state] * 3 + [slots] * 2 + [jax.ShapeDtypeStruct((2, T // 2, Dm), BF)],
        scratch_shapes=[pltpu.VMEM((T, Dm), BF), pltpu.VMEM((T, Dm), F32), pltpu.VMEM((T, Dm), F32)] + [DMA((6,))] * 4 + [DMA((2,))] * 2,
        compiler_params=params(60 * MIB, 0),
        cost_estimate=cost(8, wg),
        name="chain",
    )(x, dy, dy, wg, wu, wd)

    ft = 512
    n = ff // (SIDE * ft)
    rows = mg.shape[1]
    piece = 2 * SIDE * rows + ft // SIDE
    vm = pltpu.VMEM
    peers = SIDE * SIDE - 1
    full = lambda *shape: pl.BlockSpec(shape, lambda t: (0,) * len(shape))
    gg, gu, gd, sq, _, _ = pl.pallas_call(
        functools.partial(gradient_kernel, n, rows),
        grid=(layers * n,),
        in_specs=[ANY] * 10,
        out_specs=[tiny] * 4 + [ANY, ANY],
        out_shape=[pltpu.VMEM(m.shape, BF) for m in (mg, mu, md)]
        + [pltpu.VMEM((8, 128), F32), slots, jax.ShapeDtypeStruct((4, T // 2, Dm), BF)],
        scratch_shapes=[vm((SIDE, T, Dm), BF)] * 2
        + [vm((2, Dm, T), BF)] * 2
        + [vm((2, T, ft), BF)] * 3
        + [vm((2, 256, ft), F32)] * 2
        + [vm((Dm, ft), F32)] * 4
        + [vm((2, 3, ft, Dm), BF)]
        + [vm((3, piece, ft), BF)] * 2
        + [vm((3, piece, ft), F32)] * 2
        + [vm((3, piece, ft), BF)] * 4
        + [vm((4, piece, ft), BF), vm((4, 3, 2 * rows, ft), BF), vm((peers, 8, 128), F32)]
        + [DMA((12,)), DMA((2, 12)), DMA((6,)), DMA((6,)), DMA((4,)), DMA((4,)), DMA((3, 6)), DMA((3, 6)), DMA((4, 3)), DMA((4, 3)), DMA((peers,)), DMA((peers,))],
        compiler_params=params(59 * MIB, 1),
        cost_estimate=cost(12, wg),
        name="gradients",
    )(a2, a2s, dy, dys, a1, a1h, dh1, wg, wu, wd)

    count = sum(w.size for w in (wg, wu, wd))
    parts = 4
    shapes = lambda dt: [jax.ShapeDtypeStruct(m.shape, dt) for m in (mg, mu, md)]
    buffers = lambda dt: [vm(m.shape, dt) for m in (mg, mu, md)]
    bg, bu, bd, *moments = pl.pallas_call(
        functools.partial(update_kernel, count, parts),
        in_specs=[tiny] * 4 + [ANY] * 9,
        out_specs=[tiny] * 3 + [ANY] * 6,
        out_shape=buffers(BF) + shapes(F32) + shapes(F32),
        scratch_shapes=buffers(F32) + buffers(F32) + buffers(BF) + [DMA((3 * layers * parts, 3)), DMA((3 * layers * parts, 2))],
        compiler_params=params(46 * MIB),
        name="update",
    )(sq, gg, gu, gd, mg, mu, md, vg, vu, vd, wg, wu, wd)

    new = pl.pallas_call(
        gather_kernel,
        in_specs=[ANY] * 3,
        out_specs=[tiny] * 3,
        out_shape=[pltpu.VMEM(w.shape, BF) for w in (wg, wu, wd)],
        scratch_shapes=[DMA((3,)), DMA((3, 4, 2)), DMA((3, 4, SIDE * SIDE))],
        compiler_params=params(MIB, 2),
        cost_estimate=cost(24, wg),
        name="gather",
    )(bg, bu, bd)

    new = [
        pl.pallas_call(
            out_kernel,
            in_specs=[tiny],
            out_specs=ANY,
            out_shape=jax.ShapeDtypeStruct(w.shape, BF),
            scratch_shapes=[DMA((8,))],
            compiler_params=params(MIB),
            name="out",
        )(w)
        for w in new
    ]
    return (*new, *moments)


def solution(mesh):
    side = math.isqrt(mesh.shape["dp"])
    torus = Mesh(mesh.devices.reshape(-1, side, side), ("rep", "x", "y"))
    batch = P(("rep", "x", "y"))
    rows = P(None, ("x", "y"))
    out_rows = P("rep", ("x", "y"))
    return jax.shard_map(
        step,
        mesh=torus,
        in_specs=(batch, batch, P(), P(), P(), *[rows] * 6),
        out_specs=(P("rep"),) * 3 + (out_rows,) * 6,
        check_vma=False,
    )
```

time: 573 us -> 521 us (0.909)
  local copies, waits for them, and re-layouts: 27.3 us -> 0 us
  Pallas kernels: 545 us -> 520 us
    unnamed x17 -> x0, local copies, waits for them, and re-layouts: 27.3 us -> none
    pallas_call x1, Pallas kernels: 170 us -> 154 us  [step(): pl.pallas_call(functools.partial(gradient_kernel, n, rows), grid=(layers...]
    pallas_call x5 -> x6, Pallas kernels: 374 us -> 366 us  [the longest x1 250 us: step(): pl.pallas_call(gather_kernel, in_specs=[ANY] * 3, out_specs=[tiny] * 3, o...]
where the time goes in v2:
time: 521 us
  Pallas kernels  520 us (100%)
    pallas_call x1, Pallas kernels, step(): pl.pallas_call(gather_kernel, in_specs=[ANY] * 3, out_specs=[tiny] * 3, o...  250 us
    pallas_call x1, Pallas kernels, step(): pl.pallas_call(functools.partial(gradient_kernel, n, rows), grid=(layers...  154 us
    pallas_call x1, Pallas kernels, step(): pl.pallas_call(functools.partial(chain_kernel, steps), grid=(layers * ste...  87.2 us
    pallas_call x3, Pallas kernels, step(): pl.pallas_call(out_kernel, in_specs=[tiny], out_specs=ANY, out_shape=jax....  17.8 us
    pallas_call x1, Pallas kernels, step(): pl.pallas_call(functools.partial(update_kernel, count, parts), in_specs=[...  11 us

profile of v2, /device:TPU:96, one launch (start us, length us, event | category | flops | bytes accessed | tf_op | source)
XLA Modules:
  0.0 521.0 jit_solution(14234528097848214858)
XLA Ops:
  0.6 87.2 %chain.1 = (bf16[1024,512]{1,0:T(8,128)(2,1)}, bf16[1024,512]{1,0:T(8,128)(2,1)}, bf16[1024,512]{1,0:T(8,128)(2,1)}, bf16[3,1024,512]{2,1,0:T(8,128)(2,1)}, bf16...) custom-call(bf16[1024,512]{1,0:T(8,128)(2,1)} %bitcast.2, bf16[1024,512]{1,0:T(8,128)(2,1)} %bitcast.3, ...), custom_call_target="tpu_custom_call" | custom-call | flops 68719476736 | bytes 33554432 | tf_op jit(solution)/shard_map/chain/pallas_call | solution.py:588
  87.9 153.8 %gradients.1 = (bf16[2,32,8192]{2,1,0:T(8,128)(2,1)S(1)}, bf16[2,32,8192]{2,1,0:T(8,128)(2,1)S(1)}, bf16[2,512,512]{2,1,0:T(8,128)(2,1)S(1)}, f32[8,128]{1,0:T(8...) custom-call(bf16[1024,512]{1,0:T(8,128)(2,1)} %get-tuple-element.31.a2, ...), custom_call_target="tpu_custom_call" | custom-call | flops 103079215104 | bytes 33554432 | tf_op jit(solution)/shard_map/gradients/pallas_call | solution.py:607
  241.6 11.0 %update.1 = (bf16[2,32,8192]{2,1,0:T(8,128)(2,1)S(1)}, bf16[2,32,8192]{2,1,0:T(8,128)(2,1)S(1)}, bf16[2,512,512]{2,1,0:T(8,128)(2,1)S(1)}, f32[2,32,8192]{2,1,0:...) custom-call(f32[8,128]{1,0:T(8,128)S(1)} %get-tuple-element.37.sq, ...), custom_call_target="tpu_custom_call" | custom-call | tf_op jit(solution)/shard_map/update/pallas_call | solution.py:634
  252.6 250.4 %gather.1 = (bf16[2,512,8192]{2,1,0:T(8,128)(2,1)S(1)}, bf16[2,512,8192]{2,1,0:T(8,128)(2,1)S(1)}, bf16[2,8192,512]{2,1,0:T(8,128)(2,1)S(1)}) custom-call(bf16[2,32,8192]{2,1,0:T(8,128)(2,1)S(1)} %get-tuple-element.41.bg, bf16[2,32,8192]{2,1,0:T(8,128)(2,1)S(1)} %get-tuple-element.42.bu, bf16[2,512,512]{2,1,0:T(8,128)(2,1)S(1)} %get-tuple-element.43.bd), custom_call_target="tpu_custom_call" | custom-call | flops 206158430208 | bytes 33554432 | tf_op jit(solution)/shard_map/gather/pallas_call | solution.py:644
  503.0 5.9 %out.3 = bf16[2,512,8192]{2,1,0:T(8,128)(2,1)} custom-call(bf16[2,512,8192]{2,1,0:T(8,128)(2,1)S(1)} %get-tuple-element.44.src), custom_call_target="tpu_custom_call" | custom-call | tf_op jit(solution)/shard_map/out/pallas_call | solution.py:656
  508.9 5.9 %out.4 = bf16[2,512,8192]{2,1,0:T(8,128)(2,1)} custom-call(bf16[2,512,8192]{2,1,0:T(8,128)(2,1)S(1)} %get-tuple-element.45.src), custom_call_target="tpu_custom_call" | custom-call | tf_op jit(solution)/shard_map/out/pallas_call | solution.py:656
  514.9 5.9 %out.5 = bf16[2,8192,512]{2,1,0:T(8,128)(2,1)} custom-call(bf16[2,8192,512]{2,1,0:T(8,128)(2,1)S(1)} %get-tuple-element.46.src), custom_call_target="tpu_custom_call" | custom-call | tf_op jit(solution)/shard_map/out/pallas_call | solution.py:656

commit v3 on v2

--- a/solution.py
+++ b/solution.py
@@ -40,25 +40,49 @@
     return me, lax.rem(me + 1, SIDE), lax.rem(me + SIDE - 1, SIDE)
 
 
-def greet(peers):
+class Place:
+    def __init__(self):
+        self.turned = lax.rem(lax.axis_index("rep"), 2)
+        x, y = lax.axis_index("x"), lax.axis_index("y")
+        self.u, self.v = self.pair(x, y)
+
+    def pair(self, a, b):
+        return a + self.turned * (b - a), b + self.turned * (a - b)
+
+    def device(self, u, v):
+        x, y = self.pair(u, v)
+        return {"x": x, "y": y}
+
+    def rank(self, u, v):
+        x, y = self.pair(u, v)
+        return x * SIDE + y
+
+    def gathering(self, step):
+        return self.device(lax.rem(self.u + step, SIDE), self.v)
+
+    def summing(self, step):
+        return self.device(self.u, lax.rem(self.v + step, SIDE))
+
+
+def greet(devices):
     barrier = pltpu.get_barrier_semaphore()
-    for axis, index in peers:
-        pl.semaphore_signal(barrier, inc=1, device_id={axis: index}, device_id_type=MESH)
-    pl.semaphore_wait(barrier, len(peers))
-
-
-def remote(src, dst, send, recv, axis, index):
+    for device in devices:
+        pl.semaphore_signal(barrier, inc=1, device_id=device, device_id_type=MESH)
+    pl.semaphore_wait(barrier, len(devices))
+
+
+def remote(src, dst, send, recv, device):
     return pltpu.make_async_remote_copy(
-        src_ref=src, dst_ref=dst, send_sem=send, recv_sem=recv, device_id={axis: index}, device_id_type=MESH
+        src_ref=src, dst_ref=dst, send_sem=send, recv_sem=recv, device_id=device, device_id_type=MESH
     )
 
 
 class Gather:
-    def __init__(self, own, slots, send, recv):
-        _, after, before = ring("x")
+    def __init__(self, place, own, slots, send, recv):
+        after, before = place.gathering(1), place.gathering(SIDE - 1)
         half = own.shape[0] // 2
         top, bottom = pl.ds(0, half), pl.ds(half, half)
-        c = lambda k, src, dst, to: remote(src, dst, send.at[k], recv.at[k], "x", to)
+        c = lambda k, src, dst, to: remote(src, dst, send.at[k], recv.at[k], to)
         self.first = [
             c(0, own.at[top], slots.at[0, top], after),
             c(1, own.at[bottom], slots.at[1, bottom], before),
@@ -88,22 +112,43 @@
 
 
 def chain_kernel(
-    steps, x, dy, dy_any, wg, wu, wd, a1, a2, dh1, dys, a2s, halves, h1, accg, accu, send, recv, send2, recv2, send1, recv1
+    steps, x, dy, dy_any, wg_any, wu_any, wd_any, a1, a2, dh1, dys, a2s, halves, saved, h1, accg, accu, bg, bu, bd,
+    stage, wsem, ssem, send, recv, send2, recv2, send1, recv1,
 ):
     j = pl.program_id(0)
-    _, after, before = ring("x")
+    place = Place()
+    after, before = place.gathering(1), place.gathering(SIDE - 1)
     half = a1.shape[0] // 2
-    gather_dy = Gather(dy_any, dys, send, recv)
-    gather_a2 = Gather(a2, a2s, send2, recv2)
+    gather_dy = Gather(place, dy_any, dys, send, recv)
+    gather_a2 = Gather(place, a2, a2s, send2, recv2)
     part = [
-        remote(a1.at[pl.ds(0, half)], halves.at[0], send1.at[0], recv1.at[0], "x", after),
-        remote(a1.at[pl.ds(half, half)], halves.at[1], send1.at[1], recv1.at[1], "x", before),
+        remote(a1.at[pl.ds(0, half)], halves.at[0], send1.at[0], recv1.at[0], after),
+        remote(a1.at[pl.ds(half, half)], halves.at[1], send1.at[1], recv1.at[1], before),
     ]
-    tiles = [pl.ds(k, 256) for k in range(0, wg.shape[2], 256)]
+    ft = bg.shape[2]
+    tiles = [pl.ds(q, 256) for q in range(0, ft, 256)]
+
+    width = saved.shape[2] // SIDE
+    begin = lax.div(place.rank(place.u, 0), ft // width)
+
+    def share(k):
+        return lax.rem(k + begin, steps)
+
+    def weights(j):
+        layer, slot = lax.div(j, steps), lax.rem(j, 2)
+        step = lax.rem(j + layer * begin, steps)
+        at = pl.ds(pl.multiple_of(step * ft, ft), ft)
+        return [
+            pltpu.make_async_copy(wg_any.at[layer, :, at], bg.at[slot], wsem.at[slot, 0]),
+            pltpu.make_async_copy(wu_any.at[layer, :, at], bu.at[slot], wsem.at[slot, 1]),
+            pltpu.make_async_copy(wd_any.at[layer, at, :], bd.at[slot], wsem.at[slot, 2]),
+        ]
 
     @pl.when(j == 0)
     def _():
-        greet([("x", after), ("x", before)])
+        for copy in weights(j):
+            copy.start()
+        greet([after, before])
         gather_dy.start()
         a1[...] = normed(x[...])
         accg[...] = jnp.zeros_like(accg)
@@ -125,12 +170,38 @@
         for copy in part:
             copy.start()
 
+    k = j - steps
+
+    def kept(k, do):
+        for part in range(ft // width):
+            block = share(k) * (ft // width) + part
+            u, v = place.pair(lax.div(block, SIDE), lax.rem(block, SIDE))
+            to = pl.ds(pl.multiple_of(v * width, width), width)
+
+            @pl.when((k >= 0) & (u == place.u))
+            def _():
+                slot = lax.rem(k, 2)
+                do(pltpu.make_async_copy(stage.at[slot, :, :, pl.ds(part * width, width)], saved.at[:, :, to], ssem.at[slot, part]))
+
+    kept(k - 2, lambda copy: copy.wait())
+
+    for copy in weights(j):
+        copy.wait()
+
+    @pl.when(j < 2 * steps - 1)
+    def _():
+        for copy in weights(j + 1):
+            copy.start()
+
+    slot = lax.rem(j, 2)
+    wg, wu, wd = bg.at[pl.ds(slot, 1)], bu.at[pl.ds(slot, 1)], bd.at[pl.ds(slot, 1)]
+
     @pl.when(j < steps)
     def _():
         a = a1[...]
         hidden = []
-        for k in tiles:
-            gate, up = dot(a, wg[0, :, k]), dot(a, wu[0, :, k])
+        for q in tiles:
+            gate, up = dot(a, wg[0, :, q]), dot(a, wu[0, :, q])
             hidden.append((gate * sigmoid(gate) * up).astype(BF))
         accg[...] += dot(jnp.concatenate(hidden, 1), wd[0])
 
@@ -143,16 +214,18 @@
     @pl.when(j >= steps)
     def _():
         a, d = a2[...], dy[...]
-        by_up, by_gate = [], []
-        for k in tiles:
-            gate, up = dot(a, wg[0, :, k]), dot(a, wu[0, :, k])
-            dhid = dot_t(d, wd[0, k, :]).astype(BF).astype(F32)
+        for q in tiles:
+            gate, up = dot(a, wg[0, :, q]), dot(a, wu[0, :, q])
+            dhid = dot_t(d, wd[0, q, :]).astype(BF).astype(F32)
             s = sigmoid(gate)
             silu = gate * s
-            by_up.append((dhid * silu).astype(BF))
-            by_gate.append((dhid * up * (s + silu * (1.0 - s))).astype(BF))
-        accu[...] += dot_t(jnp.concatenate(by_up, 1), wu[0])
-        accg[...] += dot_t(jnp.concatenate(by_gate, 1), wg[0])
+            stage[slot, 0, :, q] = (silu * up).astype(BF)
+            stage[slot, 1, :, q] = (dhid * silu).astype(BF)
+            stage[slot, 2, :, q] = (dhid * up * (s + silu * (1.0 - s))).astype(BF)
+        accu[...] += dot_t(stage[slot, 1], wu[0])
+        accg[...] += dot_t(stage[slot, 2], wg[0])
+
+    kept(k, lambda copy: copy.start())
 
     @pl.when(j == 2 * steps - 1)
     def _():
@@ -161,6 +234,8 @@
         scale = lax.rsqrt(jnp.mean(wide * wide, -1, keepdims=True) + 1e-6)
         along = jnp.sum(da * wide, -1, keepdims=True) * (scale * scale * scale * (1.0 / wide.shape[-1]))
         dh1[...] = dy[...] + (da * scale - wide * along).astype(BF)
+        for back in (1, 0):
+            kept(k - back, lambda copy: copy.wait())
         gather_a2.finish()
         for copy in part:
             copy.wait()
@@ -172,29 +247,30 @@
 
 def gradient_kernel(
     n, rows,
-    a2, a2s, dy, dys, a1, a1h, dh1, wg, wu, wd,
+    a2, a2s, dy, dys, a1, a1h, dh1, wg, wu, wd, saved,
     og, ou, od, osq, dslots, b1,
-    A, D, AT, DT, hid, dg, du, silus, slopes, ag, au, ad, dT, wbuf, far, raw, keep, own, summed, frecv, rm, rp, GT, XR, others,
-    lsem, wsem, gsend, grecv, bsend, brecv, rsend, rrecv, xsend, xrecv, qsend, qrecv,
+    A, D, AT, DT, hid, dg, du, silus, slopes, ag, au, ad, dT, wbuf, far, raw, keep, own, summed, frecv, rm, rp, GT, XR, others, factors,
+    lsem, fsem, wsem, gsend, grecv, bsend, brecv, rsend, rrecv, xsend, xrecv, qsend, qrecv,
 ):
     t = pl.program_id(0)
     last = 2 * n - 1
-    x, xa, xb_ = ring("x")
-    y, ya, yb = ring("y")
+    place = Place()
+    u, v = place.u, place.v
+    after, before = place.gathering(1), place.gathering(SIDE - 1)
     T, Dm = a2.shape
     half = T // 2
     ft = wbuf.shape[2]
     chunk = ft // SIDE
     top, bottom = pl.ds(0, half), pl.ds(half, half)
-    gather = Gather(dh1, dslots, gsend, grecv)
-    bcopy = lambda k, src, to: remote(src, b1.at[k], bsend.at[k], brecv.at[k], "x", to)
-    rest = [bcopy(0, a1.at[bottom], xa), bcopy(1, a1.at[top], xb_), bcopy(2, a1h.at[0], xa), bcopy(3, a1h.at[1], xb_)]
+    gather = Gather(place, dh1, dslots, gsend, grecv)
+    bcopy = lambda k, src, to: remote(src, b1.at[k], bsend.at[k], brecv.at[k], to)
+    rest = [bcopy(0, a1.at[bottom], after), bcopy(1, a1.at[top], before), bcopy(2, a1h.at[0], after), bcopy(3, a1h.at[1], before)]
 
     def weights(t):
         layer, j, slot = 1 - lax.div(t, n), lax.rem(t, n), lax.rem(t, 2)
         out = []
         for k in range(SIDE):
-            at = pl.multiple_of(x * (n * ft) + k * ft + j * chunk, chunk)
+            at = pl.multiple_of(place.rank(u, k) * (n * chunk) + j * chunk, chunk)
             to = pl.ds(k * chunk, chunk)
             out.append(pltpu.make_async_copy(wg.at[layer, :, pl.ds(at, chunk)], wbuf.at[slot, 0, :, to], wsem.at[slot, 3 * k]))
             out.append(pltpu.make_async_copy(wu.at[layer, :, pl.ds(at, chunk)], wbuf.at[slot, 1, :, to], wsem.at[slot, 3 * k + 1]))
@@ -212,18 +288,26 @@
         + [(dslots.at[k], D.at[k + 1]) for k in range(3)]
     )
 
+    def own_factors(t):
+        out = []
+        for k in range(SIDE):
+            at = pl.multiple_of(k * (n * chunk) + t * chunk, chunk)
+            out.append(pltpu.make_async_copy(saved.at[:, :, pl.ds(at, chunk)], factors.at[:, :, pl.ds(k * chunk, chunk)], fsem.at[k]))
+        return out
+
     def reduction(t):
         s = lax.rem(t, 3)
         h = far.shape[1] // 2
         lo, hi = pl.ds(0, h), pl.ds(h, h)
-        c = lambda k, src, dst, to: remote(src, dst, rsend.at[s, k], rrecv.at[s, k], "y", to)
+        next_, last_ = place.summing(1), place.summing(SIDE - 1)
+        c = lambda k, src, dst, to: remote(src, dst, rsend.at[s, k], rrecv.at[s, k], to)
         return [
-            c(0, far.at[s, lo], frecv.at[s, lo], ya),
-            c(1, far.at[s, hi], frecv.at[s, hi], yb),
-            c(2, raw.at[s, hi], rm.at[s, hi], ya),
-            c(3, raw.at[s, lo], rp.at[s, lo], yb),
-            c(4, summed.at[s, lo], rm.at[s, lo], ya),
-            c(5, summed.at[s, hi], rp.at[s, hi], yb),
+            c(0, far.at[s, lo], frecv.at[s, lo], next_),
+            c(1, far.at[s, hi], frecv.at[s, hi], last_),
+            c(2, raw.at[s, hi], rm.at[s, hi], next_),
+            c(3, raw.at[s, lo], rp.at[s, lo], last_),
+            c(4, summed.at[s, lo], rm.at[s, lo], next_),
+            c(5, summed.at[s, hi], rp.at[s, hi], last_),
         ]
 
     def pack(t):
@@ -231,33 +315,33 @@
         dT[...] = ad[...].T
 
         def rows_for(rel):
-            yd = lax.rem(y + rel, SIDE)
+            vd = lax.rem(v + rel, SIDE)
             parts = {}
             for b in range(SIDE):
-                at = pl.multiple_of(b * (SIDE * rows) + yd * rows, rows)
+                at = pl.multiple_of(place.rank(b, vd) * rows, rows)
                 to = b * 2 * rows + (b // 2) * 4 * rows
                 parts[to] = ag[pl.ds(at, rows), :]
                 parts[to + rows] = au[pl.ds(at, rows), :]
-            at = pl.multiple_of(yd * chunk, chunk)
+            at = pl.multiple_of(vd * chunk, chunk)
             parts[4 * rows] = dT[pl.ds(at, chunk // 2), :]
             parts[6 * rows] = dT[pl.ds(at + chunk // 2, chunk // 2), :]
             return parts
 
         h = far.shape[1] // 2
-        for to, v in rows_for(2).items():
-            far[s, pl.ds(to, v.shape[0]), :] = v.astype(BF)
-        for to, v in rows_for(1).items():
+        for to, part in rows_for(2).items():
+            far[s, pl.ds(to, part.shape[0]), :] = part.astype(BF)
+        for to, part in rows_for(1).items():
             if to < h:
-                keep[s, pl.ds(to, v.shape[0]), :] = v
+                keep[s, pl.ds(to, part.shape[0]), :] = part
             else:
-                raw[s, pl.ds(to, v.shape[0]), :] = v.astype(BF)
-        for to, v in rows_for(3).items():
+                raw[s, pl.ds(to, part.shape[0]), :] = part.astype(BF)
+        for to, part in rows_for(3).items():
             if to < h:
-                raw[s, pl.ds(to, v.shape[0]), :] = v.astype(BF)
+                raw[s, pl.ds(to, part.shape[0]), :] = part.astype(BF)
             else:
-                keep[s, pl.ds(to, v.shape[0]), :] = v
-        for to, v in rows_for(0).items():
-            own[s, pl.ds(to, v.shape[0]), :] = v
+                keep[s, pl.ds(to, part.shape[0]), :] = part
+        for to, part in rows_for(0).items():
+            own[s, pl.ds(to, part.shape[0]), :] = part
 
     def total(t):
         s = lax.rem(t, 3)
@@ -271,9 +355,9 @@
     def across(t):
         out, g = [], lax.rem(t, 4)
         for r in range(1, SIDE):
-            to = lax.rem(x + r, SIDE)
+            to = lax.rem(u + r, SIDE)
             at = pl.multiple_of(gate_row(to, rows), 2 * rows)
-            out.append(remote(GT.at[g, pl.ds(at, 2 * rows)], XR.at[g, r - 1], xsend.at[g, r - 1], xrecv.at[g, r - 1], "x", to))
+            out.append(remote(GT.at[g, pl.ds(at, 2 * rows)], XR.at[g, r - 1], xsend.at[g, r - 1], xrecv.at[g, r - 1], place.device(to, v)))
         return out
 
     def final(t):
@@ -295,27 +379,24 @@
         for copy in across(t):
             copy.wait()
         for r in range(SIDE):
-            source = lax.rem(x + SIDE - r, SIDE)
+            source = lax.rem(u + SIDE - r, SIDE)
             if r:
                 piece = XR[g, r - 1]
             else:
-                piece = GT[g, pl.ds(pl.multiple_of(gate_row(x, rows), 2 * rows), 2 * rows), :]
+                piece = GT[g, pl.ds(pl.multiple_of(gate_row(u, rows), 2 * rows), 2 * rows), :]
             for k in range(SIDE):
-                at = pl.multiple_of(source * (n * ft) + k * ft + j * chunk, chunk)
+                at = pl.multiple_of(place.rank(source, k) * (n * chunk) + j * chunk, chunk)
                 og[layer, :, pl.ds(at, chunk)] = piece[:rows, k * chunk : (k + 1) * chunk]
                 ou[layer, :, pl.ds(at, chunk)] = piece[rows:, k * chunk : (k + 1) * chunk]
         od[layer, pl.ds(pl.multiple_of(j * chunk, chunk), chunk), :] = GT[g, 4 * rows : 8 * rows, :]
 
-    peers = [(lax.rem(x + i, SIDE), lax.rem(y + k, SIDE)) for i in range(SIDE) for k in range(SIDE)][1:]
+    peers = [place.device(lax.rem(u + i, SIDE), lax.rem(v + k, SIDE)) for i in range(SIDE) for k in range(SIDE)][1:]
 
     @pl.when(t == 0)
     def _():
-        for copy in first() + weights(t):
-            copy.start()
-        barrier = pltpu.get_barrier_semaphore()
-        for px, py in peers:
-            pl.semaphore_signal(barrier, inc=1, device_id={"x": px, "y": py}, device_id_type=MESH)
-        pl.semaphore_wait(barrier, len(peers))
+        for copy in first() + weights(t) + own_factors(t):
+            copy.start()
+        greet(peers)
         gather.start()
         for copy in rest:
             copy.start()
@@ -338,10 +419,6 @@
 
     slot = lax.rem(t, 2)
     sub = silus.shape[1]
-    ag[...] = jnp.zeros_like(ag)
-    au[...] = jnp.zeros_like(au)
-    ad[...] = jnp.zeros_like(ad)
-
     def chain(s, b):
         AT[b] = A[s].T
         DT[b] = D[s].T
@@ -367,11 +444,33 @@
         au[...] += dot(AT[b], du[b])
         ad[...] += dot(DT[b], hid[b])
 
-    for s in range(SIDE):
+    @pl.when(t < n)
+    def _():
+        for copy in own_factors(t):
+            copy.wait()
+        AT[0] = A[0].T
+        DT[0] = D[0].T
+        ag[...] = dot(AT[0], factors[2])
+        au[...] = dot(AT[0], factors[1])
+        ad[...] = dot(DT[0], factors[0])
+
+    @pl.when(t < n - 1)
+    def _():
+        for copy in own_factors(t + 1):
+            copy.start()
+
+    @pl.when(t >= n)
+    def _():
+        chain(0, 0)
+        ag[...] = dot(AT[0], dg[0])
+        au[...] = dot(AT[0], du[0])
+        ad[...] = dot(DT[0], hid[0])
+
+    for s in range(1, SIDE):
         chain(s, s % 2)
-        if s:
+        if s > 1:
             contract((s - 1) % 2)
-        if s == 1:
+        if s == 2:
             pl.when(t >= 1)(functools.partial(total, t - 1))
     contract((SIDE - 1) % 2)
 
@@ -386,10 +485,6 @@
     @pl.when(t == 0)
     def _():
         gather.relay()
-
-    @pl.when(t >= 3)
-    def _():
-        assemble(t - 3)
 
     @pl.when(t >= 2)
     def _():
@@ -398,6 +493,11 @@
     pack(t)
     for copy in reduction(t)[:4]:
         copy.start()
+
+    @pl.when(t >= 3)
+    def _():
+        assemble(t - 3)
+
 
     @pl.when(t == last)
     def _():
@@ -405,12 +505,7 @@
         total(t)
         assemble(t - 2)
         final(t)
-        copies = [
-            pltpu.make_async_remote_copy(
-                src_ref=osq, dst_ref=others.at[k], send_sem=qsend.at[k], recv_sem=qrecv.at[k], device_id={"x": px, "y": py}, device_id_type=MESH
-            )
-            for k, (px, py) in enumerate(peers)
-        ]
+        copies = [remote(osq, others.at[k], qsend.at[k], qrecv.at[k], peer) for k, peer in enumerate(peers)]
         for copy in copies:
             copy.start()
         assemble(t - 1)
@@ -424,51 +519,56 @@
 
 
 def fold(v):
-    out = None
-    for i in range(v.shape[0] // 8):
-        for k in range(v.shape[1] // 128):
-            tile = v[i * 8 : i * 8 + 8, k * 128 : k * 128 + 128]
-            out = tile if out is None else out + tile
-    return out
+    tiles = [v[i : i + 8, k : k + 128] for i in range(0, v.shape[0], 8) for k in range(0, v.shape[1], 128)]
+    while len(tiles) > 1:
+        tiles = [a + b for a, b in zip(tiles[::2], tiles[1::2])] + tiles[len(tiles) // 2 * 2 :]
+    return tiles[0]
 
 
 def update_kernel(count, parts, sq, *refs):
     g, m, v, w, nw, nm, nv, bm, bv, bw = (refs[3 * i : 3 * i + 3] for i in range(10))
     came, left = refs[30:]
     mine = lax.axis_index("x") * SIDE + lax.axis_index("y")
-    pieces = [(i, l, c) for i in range(3) for l in range(g[0].shape[0]) for c in range(parts)]
-
-    def at(i, l, c, first=0):
+    pieces = g[0].shape[0] * parts
+
+    def at(i, k, first=0):
         _, rows, width = g[i].shape
+        l, c = lax.div(k, parts), lax.rem(k, parts)
         if i < 2:
-            return (l, pl.ds(first, rows), pl.ds(c * (width // parts), width // parts))
-        return (l, pl.ds(first + c * (rows // parts), rows // parts), slice(None))
-
-    def arrivals(k):
-        i, l, c = pieces[k]
-        here = at(i, l, c)
-        there = at(i, l, c, pl.multiple_of(mine * g[i].shape[1], g[i].shape[1]))
+            return (l, pl.ds(first, rows), pl.ds(pl.multiple_of(c * (width // parts), width // parts), width // parts))
+        return (l, pl.ds(pl.multiple_of(first + c * (rows // parts), rows // parts), rows // parts), slice(None))
+
+    def arrivals(i, k):
+        here, there = at(i, k), at(i, k, pl.multiple_of(mine * g[i].shape[1], g[i].shape[1]))
         return [
-            pltpu.make_async_copy(m[i].at[here], bm[i].at[here], came.at[k, 0]),
-            pltpu.make_async_copy(v[i].at[here], bv[i].at[here], came.at[k, 1]),
-            pltpu.make_async_copy(w[i].at[there], bw[i].at[here], came.at[k, 2]),
+            pltpu.make_async_copy(m[i].at[here], bm[i].at[here], came.at[i, k, 0]),
+            pltpu.make_async_copy(v[i].at[here], bv[i].at[here], came.at[i, k, 1]),
+            pltpu.make_async_copy(w[i].at[there], bw[i].at[here], came.at[i, k, 2]),
         ]
 
-    def departures(k):
-        i, l, c = pieces[k]
-        here = at(i, l, c)
+    def departures(i, k):
+        here = at(i, k)
         return [
-            pltpu.make_async_copy(bm[i].at[here], nm[i].at[here], left.at[k, 0]),
-            pltpu.make_async_copy(bv[i].at[here], nv[i].at[here], left.at[k, 1]),
+            pltpu.make_async_copy(bm[i].at[here], nm[i].at[here], left.at[i, k, 0]),
+            pltpu.make_async_copy(bv[i].at[here], nv[i].at[here], left.at[i, k, 1]),
         ]
 
-    for k in range(len(pieces)):
-        for copy in arrivals(k):
-            copy.start()
-    factor = jnp.minimum(1.0, 0.5 * lax.rsqrt(jnp.sum(sq[...], keepdims=True) / count + 1e-30))
-    for k, (i, l, c) in enumerate(pieces):
-        here = at(i, l, c)
-        for copy in arrivals(k):
+    def each(do):
+        for i in range(3):
+
+            def one(k, _, i=i):
+                do(i, k)
+                return 0
+
+            lax.fori_loop(0, pieces, one, 0)
+
+    def come(i, k):
+        for copy in arrivals(i, k):
+            copy.start()
+
+    def work(i, k):
+        here = at(i, k)
+        for copy in arrivals(i, k):
             copy.wait()
         grad = g[i][here].astype(F32) * factor
         new_m = 0.9 * bm[i][here] + 0.1 * grad
@@ -478,17 +578,23 @@
         nw[i][here] = (wide - 0.02 * step).astype(BF)
         bm[i][here] = new_m
         bv[i][here] = new_v
-        for copy in departures(k):
-            copy.start()
-    for k in range(len(pieces)):
-        for copy in departures(k):
-            copy.wait()
+        for copy in departures(i, k):
+            copy.start()
+
+    def leave(i, k):
+        for copy in departures(i, k):
+            copy.wait()
+
+    each(come)
+    factor = jnp.minimum(1.0, 0.5 * lax.rsqrt(jnp.sum(sq[...], keepdims=True) / count + 1e-30))
+    each(work)
+    each(leave)
 
 
 def gather_kernel(bg, bu, bd, og, ou, od, local, send, recv):
     x, xa, xb = ring("x")
     y, ya, yb = ring("y")
-    greet([("x", xa), ("x", xb), ("y", ya), ("y", yb)])
+    greet([{"x": xa}, {"x": xb}, {"y": ya}, {"y": yb}])
     colours = [("x", xa, "y", ya, -1), ("x", xb, "y", yb, 1), ("y", ya, "x", xa, -1), ("y", yb, "x", xb, 1)]
     blocks, outs = (bg, bu, bd), (og, ou, od)
 
@@ -519,7 +625,7 @@
         i2, j2 = (i + 1, j) if along == 0 else (i, j + 1)
         return remote(
             source(piece, colour, i, j), place(piece, colour, owner(colour, i, j)),
-            send.at[piece, colour, along], recv.at[piece, colour, i2 * SIDE + j2], a if along == 0 else b, an if along == 0 else bn,
+            send.at[piece, colour, along], recv.at[piece, colour, i2 * SIDE + j2], {a: an} if along == 0 else {b: bn},
         )
 
     mine = x * SIDE + y
@@ -583,15 +689,20 @@
     tiny = pl.BlockSpec(memory_space=pltpu.VMEM)
     ft = 1024
     steps = ff // ft
-    across = pl.BlockSpec((1, Dm, ft), lambda j: (lax.div(j, steps), 0, lax.rem(j, steps)))
-    down = pl.BlockSpec((1, ft, Dm), lambda j: (lax.div(j, steps), lax.rem(j, steps), 0))
-    a1, a2, dh1, dys, a2s, a1h = pl.pallas_call(
+    a1, a2, dh1, dys, a2s, a1h, saved = pl.pallas_call(
         functools.partial(chain_kernel, steps),
         grid=(layers * steps,),
-        in_specs=[whole, whole, ANY, across, across, down],
-        out_specs=[whole] * 3 + [ANY] * 3,
-        out_shape=[state] * 3 + [slots] * 2 + [jax.ShapeDtypeStruct((2, T // 2, Dm), BF)],
-        scratch_shapes=[pltpu.VMEM((T, Dm), BF), pltpu.VMEM((T, Dm), F32), pltpu.VMEM((T, Dm), F32)] + [DMA((6,))] * 4 + [DMA((2,))] * 2,
+        in_specs=[whole, whole] + [ANY] * 4,
+        out_specs=[whole] * 3 + [ANY] * 4,
+        out_shape=[state] * 3
+        + [slots] * 2
+        + [jax.ShapeDtypeStruct((2, T // 2, Dm), BF), jax.ShapeDtypeStruct((3, T, ff // SIDE), BF)],
+        scratch_shapes=[pltpu.VMEM((T, Dm), BF)]
+        + [pltpu.VMEM((T, Dm), F32)] * 2
+        + [pltpu.VMEM((2, Dm, ft), BF)] * 2
+        + [pltpu.VMEM((2, ft, Dm), BF), pltpu.VMEM((2, 3, T, ft), BF), DMA((2, 3)), DMA((2, 2))]
+        + [DMA((6,))] * 4
+        + [DMA((2,))] * 2,
         compiler_params=params(60 * MIB, 0),
         cost_estimate=cost(8, wg),
         name="chain",
@@ -607,7 +718,7 @@
     gg, gu, gd, sq, _, _ = pl.pallas_call(
         functools.partial(gradient_kernel, n, rows),
         grid=(layers * n,),
-        in_specs=[ANY] * 10,
+        in_specs=[ANY] * 11,
         out_specs=[tiny] * 4 + [ANY, ANY],
         out_shape=[pltpu.VMEM(m.shape, BF) for m in (mg, mu, md)]
         + [pltpu.VMEM((8, 128), F32), slots, jax.ShapeDtypeStruct((4, T // 2, Dm), BF)],
@@ -620,12 +731,12 @@
         + [vm((3, piece, ft), BF)] * 2
         + [vm((3, piece, ft), F32)] * 2
         + [vm((3, piece, ft), BF)] * 4
-        + [vm((4, piece, ft), BF), vm((4, 3, 2 * rows, ft), BF), vm((peers, 8, 128), F32)]
-        + [DMA((12,)), DMA((2, 12)), DMA((6,)), DMA((6,)), DMA((4,)), DMA((4,)), DMA((3, 6)), DMA((3, 6)), DMA((4, 3)), DMA((4, 3)), DMA((peers,)), DMA((peers,))],
+        + [vm((4, piece, ft), BF), vm((4, 3, 2 * rows, ft), BF), vm((peers, 8, 128), F32), vm((3, T, ft), BF)]
+        + [DMA((12,)), DMA((SIDE,)), DMA((2, 12)), DMA((6,)), DMA((6,)), DMA((4,)), DMA((4,)), DMA((3, 6)), DMA((3, 6)), DMA((4, 3)), DMA((4, 3)), DMA((peers,)), DMA((peers,))],
         compiler_params=params(59 * MIB, 1),
         cost_estimate=cost(12, wg),
         name="gradients",
-    )(a2, a2s, dy, dys, a1, a1h, dh1, wg, wu, wd)
+    )(a2, a2s, dy, dys, a1, a1h, dh1, wg, wu, wd, saved)
 
     count = sum(w.size for w in (wg, wu, wd))
     parts = 4
@@ -636,7 +747,7 @@
         in_specs=[tiny] * 4 + [ANY] * 9,
         out_specs=[tiny] * 3 + [ANY] * 6,
         out_shape=buffers(BF) + shapes(F32) + shapes(F32),
-        scratch_shapes=buffers(F32) + buffers(F32) + buffers(BF) + [DMA((3 * layers * parts, 3)), DMA((3 * layers * parts, 2))],
+        scratch_shapes=buffers(F32) + buffers(F32) + buffers(BF) + [DMA((3, layers * parts, 3)), DMA((3, layers * parts, 2))],
         compiler_params=params(46 * MIB),
         name="update",
     )(sq, gg, gu, gd, mg, mu, md, vg, vu, vd, wg, wu, wd)

time: 521 us -> 517 us (level)
    pallas_call x1, Pallas kernels: 154 us -> 144 us  [step(): pl.pallas_call(functools.partial(gradient_kernel, n, rows), grid=(layers...]
    pallas_call x1, Pallas kernels: 250 us -> 257 us  [step(): pl.pallas_call(gather_kernel, in_specs=[ANY] * 3, out_specs=[tiny] * 3, o...]
where the time goes in v3:
time: 517 us
  Pallas kernels  516 us (100%)
    pallas_call x1, Pallas kernels, step(): pl.pallas_call(gather_kernel, in_specs=[ANY] * 3, out_specs=[tiny] * 3, o...  257 us
    pallas_call x1, Pallas kernels, step(): pl.pallas_call(functools.partial(gradient_kernel, n, rows), grid=(layers...  144 us
    pallas_call x1, Pallas kernels, step(): pl.pallas_call(functools.partial(chain_kernel, steps), grid=(layers * ste...  86.3 us
    pallas_call x3, Pallas kernels, step(): pl.pallas_call(out_kernel, in_specs=[tiny], out_specs=ANY, out_shape=jax....  17.8 us
    pallas_call x1, Pallas kernels, step(): pl.pallas_call(functools.partial(update_kernel, count, parts), in_specs=[...  11 us

profile of v3, /device:TPU:96, one launch (start us, length us, event | category | flops | bytes accessed | tf_op | source)
XLA Modules:
  0.0 516.8 jit_solution(16245980653564380568)
XLA Ops:
  0.6 86.3 %chain.1 = (bf16[1024,512]{1,0:T(8,128)(2,1)}, bf16[1024,512]{1,0:T(8,128)(2,1)}, bf16[1024,512]{1,0:T(8,128)(2,1)}, bf16[3,1024,512]{2,1,0:T(8,128)(2,1)}, bf16...) custom-call(bf16[1024,512]{1,0:T(8,128)(2,1)} %bitcast.2, ...), custom_call_target="tpu_custom_call" | custom-call | flops 68719476736 | bytes 33554432 | tf_op jit(solution)/shard_map/chain/pallas_call | solution.py:692
  87.0 143.9 %gradients.1 = (bf16[2,32,8192]{2,1,0:T(8,128)(2,1)S(1)}, bf16[2,32,8192]{2,1,0:T(8,128)(2,1)S(1)}, bf16[2,512,512]{2,1,0:T(8,128)(2,1)S(1)}, f32[8,128]{1,0:T(8...) custom-call(bf16[1024,512]{1,0:T(8,128)(2,1)} %get-tuple-element.32.a2, ...), custom_call_target="tpu_custom_call" | custom-call | flops 103079215104 | bytes 33554432 | tf_op jit(solution)/shard_map/gradients/pallas_call | solution.py:718
  230.9 11.0 %update.1 = (bf16[2,32,8192]{2,1,0:T(8,128)(2,1)S(1)}, bf16[2,32,8192]{2,1,0:T(8,128)(2,1)S(1)}, bf16[2,512,512]{2,1,0:T(8,128)(2,1)S(1)}, f32[2,32,8192]{2,1,0:...) custom-call(f32[8,128]{1,0:T(8,128)S(1)} %get-tuple-element.39.sq, ...), custom_call_target="tpu_custom_call" | custom-call | tf_op jit(solution)/shard_map/update/pallas_call | solution.py:745
  241.9 257.0 %gather.1 = (bf16[2,512,8192]{2,1,0:T(8,128)(2,1)S(1)}, bf16[2,512,8192]{2,1,0:T(8,128)(2,1)S(1)}, bf16[2,8192,512]{2,1,0:T(8,128)(2,1)S(1)}) custom-call(bf16[2,32,8192]{2,1,0:T(8,128)(2,1)S(1)} %get-tuple-element.43.bg, bf16[2,32,8192]{2,1,0:T(8,128)(2,1)S(1)} %get-tuple-element.44.bu, bf16[2,512,512]{2,1,0:T(8,128)(2,1)S(1)} %get-tuple-element.45.bd), custom_call_target="tpu_custom_call" | custom-call | flops 206158430208 | bytes 33554432 | tf_op jit(solution)/shard_map/gather/pallas_call | solution.py:755
  498.9 5.9 %out.3 = bf16[2,512,8192]{2,1,0:T(8,128)(2,1)} custom-call(bf16[2,512,8192]{2,1,0:T(8,128)(2,1)S(1)} %get-tuple-element.46.src), custom_call_target="tpu_custom_call" | custom-call | tf_op jit(solution)/shard_map/out/pallas_call | solution.py:767
  504.8 5.9 %out.4 = bf16[2,512,8192]{2,1,0:T(8,128)(2,1)} custom-call(bf16[2,512,8192]{2,1,0:T(8,128)(2,1)S(1)} %get-tuple-element.47.src), custom_call_target="tpu_custom_call" | custom-call | tf_op jit(solution)/shard_map/out/pallas_call | solution.py:767
  510.7 5.9 %out.5 = bf16[2,8192,512]{2,1,0:T(8,128)(2,1)} custom-call(bf16[2,8192,512]{2,1,0:T(8,128)(2,1)S(1)} %get-tuple-element.48.src), custom_call_target="tpu_custom_call" | custom-call | tf_op jit(solution)/shard_map/out/pallas_call | solution.py:767

commit v4 on v3

--- a/solution.py
+++ b/solution.py
@@ -401,12 +401,12 @@
         for copy in rest:
             copy.start()
         osq[...] = jnp.zeros_like(osq)
-        for copy in first():
+        for copy in first()[:2]:
             copy.wait()
 
     @pl.when(t == n)
     def _():
-        for copy in second():
+        for copy in second()[:2]:
             copy.wait()
 
     for copy in weights(t):
@@ -465,6 +465,16 @@
         ag[...] = dot(AT[0], dg[0])
         au[...] = dot(AT[0], du[0])
         ad[...] = dot(DT[0], hid[0])
+
+    @pl.when(t == 0)
+    def _():
+        for copy in first()[2:]:
+            copy.wait()
+
+    @pl.when(t == n)
+    def _():
+        for copy in second()[2:]:
+            copy.wait()
 
     for s in range(1, SIDE):
         chain(s, s % 2)
@@ -739,7 +749,7 @@
     )(a2, a2s, dy, dys, a1, a1h, dh1, wg, wu, wd, saved)
 
     count = sum(w.size for w in (wg, wu, wd))
-    parts = 4
+    parts = 1
     shapes = lambda dt: [jax.ShapeDtypeStruct(m.shape, dt) for m in (mg, mu, md)]
     buffers = lambda dt: [vm(m.shape, dt) for m in (mg, mu, md)]
     bg, bu, bd, *moments = pl.pallas_call(

time: 517 us -> 514 us (level)
  no operation moved by 1% of the time
where the time goes in v4:
time: 514 us
  Pallas kernels  513 us (100%)
    pallas_call x1, Pallas kernels, step(): pl.pallas_call(gather_kernel, in_specs=[ANY] * 3, out_specs=[tiny] * 3, o...  257 us
    pallas_call x1, Pallas kernels, step(): pl.pallas_call(functools.partial(gradient_kernel, n, rows), grid=(layers...  142 us
    pallas_call x1, Pallas kernels, step(): pl.pallas_call(functools.partial(chain_kernel, steps), grid=(layers * ste...  86.3 us
    pallas_call x3, Pallas kernels, step(): pl.pallas_call(out_kernel, in_specs=[tiny], out_specs=ANY, out_shape=jax....  17.8 us
    pallas_call x1, Pallas kernels, step(): pl.pallas_call(functools.partial(update_kernel, count, parts), in_specs=[...  10.3 us

profile of v4, /device:TPU:96, one launch (start us, length us, event | category | flops | bytes accessed | tf_op | source)
XLA Modules:
  0.0 514.4 jit_solution(9209329120502906966)
XLA Ops:
  0.6 86.3 %chain.1 = (bf16[1024,512]{1,0:T(8,128)(2,1)}, bf16[1024,512]{1,0:T(8,128)(2,1)}, bf16[1024,512]{1,0:T(8,128)(2,1)}, bf16[3,1024,512]{2,1,0:T(8,128)(2,1)}, bf16...) custom-call(bf16[1024,512]{1,0:T(8,128)(2,1)} %bitcast.2, ...), custom_call_target="tpu_custom_call" | custom-call | flops 68719476736 | bytes 33554432 | tf_op jit(solution)/shard_map/chain/pallas_call | solution.py:702
  87.0 142.1 %gradients.1 = (bf16[2,32,8192]{2,1,0:T(8,128)(2,1)S(1)}, bf16[2,32,8192]{2,1,0:T(8,128)(2,1)S(1)}, bf16[2,512,512]{2,1,0:T(8,128)(2,1)S(1)}, f32[8,128]{1,0:T(8...) custom-call(bf16[1024,512]{1,0:T(8,128)(2,1)} %get-tuple-element.32.a2, ...), custom_call_target="tpu_custom_call" | custom-call | flops 103079215104 | bytes 33554432 | tf_op jit(solution)/shard_map/gradients/pallas_call | solution.py:728
  229.1 10.3 %update.1 = (bf16[2,32,8192]{2,1,0:T(8,128)(2,1)S(1)}, bf16[2,32,8192]{2,1,0:T(8,128)(2,1)S(1)}, bf16[2,512,512]{2,1,0:T(8,128)(2,1)S(1)}, f32[2,32,8192]{2,1,0:...) custom-call(f32[8,128]{1,0:T(8,128)S(1)} %get-tuple-element.39.sq, ...), custom_call_target="tpu_custom_call" | custom-call | tf_op jit(solution)/shard_map/update/pallas_call | solution.py:755
  239.4 257.0 %gather.1 = (bf16[2,512,8192]{2,1,0:T(8,128)(2,1)S(1)}, bf16[2,512,8192]{2,1,0:T(8,128)(2,1)S(1)}, bf16[2,8192,512]{2,1,0:T(8,128)(2,1)S(1)}) custom-call(bf16[2,32,8192]{2,1,0:T(8,128)(2,1)S(1)} %get-tuple-element.43.bg, bf16[2,32,8192]{2,1,0:T(8,128)(2,1)S(1)} %get-tuple-element.44.bu, bf16[2,512,512]{2,1,0:T(8,128)(2,1)S(1)} %get-tuple-element.45.bd), custom_call_target="tpu_custom_call" | custom-call | flops 206158430208 | bytes 33554432 | tf_op jit(solution)/shard_map/gather/pallas_call | solution.py:765
  496.4 5.9 %out.3 = bf16[2,512,8192]{2,1,0:T(8,128)(2,1)} custom-call(bf16[2,512,8192]{2,1,0:T(8,128)(2,1)S(1)} %get-tuple-element.46.src), custom_call_target="tpu_custom_call" | custom-call | tf_op jit(solution)/shard_map/out/pallas_call | solution.py:777
  502.3 5.9 %out.4 = bf16[2,512,8192]{2,1,0:T(8,128)(2,1)} custom-call(bf16[2,512,8192]{2,1,0:T(8,128)(2,1)S(1)} %get-tuple-element.47.src), custom_call_target="tpu_custom_call" | custom-call | tf_op jit(solution)/shard_map/out/pallas_call | solution.py:777
  508.2 5.9 %out.5 = bf16[2,8192,512]{2,1,0:T(8,128)(2,1)} custom-call(bf16[2,8192,512]{2,1,0:T(8,128)(2,1)S(1)} %get-tuple-element.48.src), custom_call_target="tpu_custom_call" | custom-call | tf_op jit(solution)/shard_map/out/pallas_call | solution.py:777
